TPU v7x, 1024 devices: a whole 4x4x32 slice. The times are simulated.
1024 devices in a mesh: cols: 128 (over z, y), chan: 8 (over x, core).
Axes of the slice: x: 4, y: 4, z: 32, core: 2. Of those that a mesh axis runs over, the one named last changes fastest.
Arguments:
- anomaly: bfloat16 [32768, 80, 128], P('cols'), may hold values from -6 to 6
- jacobian: bfloat16 [16384, 256, 128], P(('cols', 'chan')), may hold values from -0.5 to 0.5
- foot_cols: int32 [16384, 4], P('cols'), may hold values from 0 to 32767, as said below
- foot_weight: float32 [16384, 4], P('cols'), may hold values from 0.1 to 1
- obs_count: int32 [128], P('cols'), may hold values from 32 to 128, as said below
- obs_weight: bfloat16 [256, 16384], P(None, ('cols', 'chan')), may hold values from 0.25 to 4
Outputs:
- radiance_pert: bfloat16 [80, 256, 16384], P(None, 'chan', 'cols')
- ensemble_gram: float32 [1024, 80, 80], P('cols', 'chan')
Inputs may be any that keep to these rules, and one draw needn't show every extreme that they name: `foot_cols`: the footprint columns of an observation of tile t lie among the columns t * 256 - 32 to (t + 1) * 256 + 31, taken modulo 32768. The live observations of tile t are its first obs_count[t] slots; in every draw at least one tile has all 128 slots live.
All inputs are finite; a program needn't handle non-finite values.
Results may differ from a plain program's by a relative error of at most 0.0095.
Values may be sent and summed in bfloat16 or wider, within the bound.
No kernel may reach another device: no remote copies, remote signals or barrier semaphores. Data moves between devices by JAX's collectives and lax.ppermute only.
A program may use at most 32 MiB of HBM per device.

v0:
```python
import jax
import jax.numpy as jnp
from jax import lax
from jax.sharding import PartitionSpec as P

CH = 256
OBS_DEV = 128
HALO = 32
PTS = 8


def extended_2(block, sides, width):
    for axis, dim in sides:
        count = lax.axis_size(axis)
        forward = [(i, i + 1) for i in range(count - 1)]
        forward.append((count - 1, 0))
        backward = [(target, source) for source, target in forward]
        low = lax.ppermute(
            lax.slice_in_dim(block, block.shape[dim] - width, None, axis=dim), axis, forward
        )
        high = lax.ppermute(lax.slice_in_dim(block, 0, width, axis=dim), axis, backward)
        block = jnp.concatenate([low, block, high], axis=dim)
    return block


def cut_along(array, dim, devices):
    dims = array.shape
    pieces = array.reshape(*dims[:dim], devices, dims[dim] // devices, *dims[dim + 1 :])
    return jnp.moveaxis(pieces, dim, 0)


def sent_and_summed(array, axis, dim):
    pieces = cut_along(array, dim, lax.axis_size(axis))
    arrived = lax.all_to_all(pieces, axis, split_axis=0, concat_axis=0, tiled=True)
    return arrived.astype(jnp.float32).sum(axis=0)


def taper(distance, half_width):
    relative = jnp.abs(distance) / half_width
    near_part = (
        ((-0.25 * relative + 0.5) * relative + 0.625) * relative - 5.0 / 3.0
    ) * relative * relative + 1.0
    bounded = jnp.maximum(relative, 1.0)
    far_part = (
        ((((relative / 12.0 - 0.5) * relative + 0.625) * relative + 5.0 / 3.0) * relative - 5.0)
        * relative
        + 4.0
        - 2.0 / (3.0 * bounded)
    )
    return jnp.where(relative <= 1.0, near_part, jnp.where(relative <= 2.0, far_part, 0.0))


def local_gram(perturbed, error_weight, centers, tile_cols):
    spacing = tile_cols / PTS
    points = (jnp.arange(PTS, dtype=jnp.float32) + 0.5) * spacing
    locality = taper(centers[None, :] - points[:, None], spacing)
    weighted = perturbed.astype(jnp.float32) * error_weight.astype(jnp.float32)
    flat_values = perturbed.reshape(perturbed.shape[0], -1)
    gram_list = []
    for point_index in range(PTS):
        scaled = (weighted * locality[point_index][None, None, :]).astype(jnp.bfloat16)
        flat_scaled = scaled.reshape(perturbed.shape[0], -1)
        gram_list.append(
            jnp.einsum("mx,kx->mk", flat_scaled, flat_values, preferred_element_type=jnp.float32)
        )
    return jnp.stack(gram_list) / (CH * OBS_DEV)


def shards(anomaly, jacobian, foot_cols, foot_weight, obs_count, obs_weight):
    col_groups = lax.axis_size("cols")
    tile_index = lax.axis_index("cols")
    chan_index = lax.axis_index("chan")
    tile_cols = anomaly.shape[0]
    obs_share = jacobian.shape[0]
    extended = extended_2(anomaly, (("cols", 0),), HALO)
    offsets = jnp.mod(foot_cols - tile_index * tile_cols + HALO, tile_cols * col_groups)
    centers = jnp.sum(foot_weight * (offsets - HALO).astype(jnp.float32), axis=1) / jnp.sum(
        foot_weight, axis=1
    )
    first_obs = chan_index * obs_share
    own_offsets = lax.dynamic_slice_in_dim(offsets, first_obs, obs_share, 0)
    own_gains = lax.dynamic_slice_in_dim(foot_weight, first_obs, obs_share, 0)
    mixed_cols = jnp.zeros((obs_share, anomaly.shape[1], anomaly.shape[2]), jnp.float32)
    for column_slot in range(own_offsets.shape[1]):
        mixed_cols = mixed_cols + own_gains[:, column_slot, None, None] * extended[
            own_offsets[:, column_slot]
        ].astype(jnp.float32)
    mixed_cols = mixed_cols.astype(jnp.bfloat16)
    radiance = jnp.einsum("ncl,nml->mcn", jacobian, mixed_cols, preferred_element_type=jnp.float32)
    slot_numbers = first_obs + jnp.arange(obs_share, dtype=jnp.int32)
    live_mask = (slot_numbers < obs_count[0]).astype(jnp.float32)
    perturbed = (radiance * live_mask[None, None, :]).astype(jnp.bfloat16)
    error_weight = obs_weight[None]
    own_centers = lax.dynamic_slice_in_dim(centers, first_obs, obs_share, 0)
    partial_gram = local_gram(perturbed, error_weight, own_centers, tile_cols)
    received = lax.all_to_all(perturbed, "chan", split_axis=1, concat_axis=2, tiled=True)
    gram_rows = sent_and_summed(partial_gram.astype(jnp.bfloat16), "chan", 1)
    return (received, gram_rows)


def solution(mesh):
    return jax.shard_map(
        shards,
        mesh=mesh,
        in_specs=(
            P("cols", None, None),
            P(("cols", "chan"), None, None),
            P("cols", None),
            P("cols", None),
            P("cols"),
            P(None, ("cols", "chan")),
        ),
        out_specs=(P(None, "chan", "cols"), P("cols", "chan", None)),
        check_vma=False,
    )
```

profile of v0, /device:TPU:1, one launch (start us, length us, event | category | flops | bytes accessed | tf_op | source)
XLA Modules:
  0.0 97.7 jit_solution(9501298088994586203)
XLA Ops:
  0.6 0.0 copy-start
  0.6 0.0 copy-start.2
  0.7 0.0 copy-start.3
  0.7 0.0 copy-start.1
  0.7 1.5 %fusion.32 = (bf16[32,80,128]{2,1,0:T(8,128)(2,1)S(1)}, bf16[32,80,128]{2,1,0:T(8,128)(2,1)S(1)}) fusion(bf16[256,80,128]{2,1,0:T(8,128)(2,1)} %param.6), kind=kLoop, calls=%fused_computation.100 | loop fusion | bytes 2621440 | tf_op jit(solution)/shard_map/slice | solution.py:21
  2.1 4.0 %collective-permute-start = (bf16[32,80,128]{2,1,0:T(8,128)(2,1)S(1)}, bf16[32,80,128]{2,1,0:T(8,128)(2,1)}, u32[]{:S(2)}, u32[]{:S(2)}) collective-permute-start(bf16[32,80,128]{2,1,0:T(8,128)(2,1)S(1)} %get-tuple-element.10), channel_id=1, source_target_pairs={{0,8},{8,16},{16,24},{24,32},{32,40},{40,48},{48,56},{56,64},{64,7... | collective-permute-start | bytes 1966088 | tf_op jit(solution)/shard_map/ppermute | solution.py:18
  6.2 19.6 %collective-permute-start.1 = (bf16[32,80,128]{2,1,0:T(8,128)(2,1)S(1)}, bf16[32,80,128]{2,1,0:T(8,128)(2,1)S(1)}, u32[]{:S(2)}, u32[]{:S(2)}) collective-permute-start(bf16[32,80,128]{2,1,0:T(8,128)(2,1)S(1)} %get-tuple-element.9), channel_id=1, source_target_pairs={{8,0},{16,8},{24,16},{32,24},{40,32},{48,40},{56,48},{64,56},{72,6... | collective-permute-start | bytes 1966088 | tf_op jit(solution)/shard_map/ppermute | solution.py:21
  26.4 0.0 copy-done.2
  26.4 0.1 constant_dynamic-slice_fusion.1
  26.5 0.0 copy-done.3
  26.5 0.1 constant_dynamic-slice_fusion
  26.6 0.1 dynamic_slice.11
  26.7 0.0 copy-done.1
  26.7 0.1 fusion.24
  26.8 11.5 %collective-permute-done = bf16[32,80,128]{2,1,0:T(8,128)(2,1)} collective-permute-done((bf16[32,80,128]{2,1,0:T(8,128)(2,1)S(1)}, bf16[32,80,128]{2,1,0:T(8,128)(2,1)}, u32[]{:S(2)}, u32[]{:S(2)}) %collective-permute-start) | collective-permute-done | bytes 655392 | tf_op jit(solution)/shard_map/ppermute | solution.py:18
  38.3 2.0 %constant_dynamic-update-slice_fusion.2 = bf16[320,80,128]{2,1,0:T(8,128)(2,1)} fusion(bf16[32,80,128]{2,1,0:T(8,128)(2,1)} %collective-permute-done), kind=kLoop, calls=%fused_computation.50 | loop fusion | bytes 1310720
  40.3 5.7 %constant_dynamic-update-slice_fusion.1 = bf16[320,80,128]{2,1,0:T(8,128)(2,1)} fusion(bf16[320,80,128]{2,1,0:T(8,128)(2,1)} %constant_dynamic-update-slice_fusion.2, bf16[256,80,128]{2,1,0:T(8,128)(2,1)} %param.6), kind=kLoop, calls=%fused_computation.49 | loop fusion | bytes 10485760
  46.0 0.0 collective-permute-done.1
  46.0 0.9 constant_dynamic-update-slice_fusion
  46.9 3.5 %gather_fusion.3 = bf16[16,80,128]{2,1,0:T(8,128)(2,1)S(1)} fusion(bf16[320,80,128]{2,1,0:T(8,128)(2,1)} %constant_dynamic-update-slice_fusion, s32[1024]{0:T(1024)S(1)} %get-tuple-element.27), kind=kCustom, calls=%fused_computation.3 | custom fusion | bytes 655424 | tf_op jit(solution)/shard_map/gather | solution.py:85
  50.4 3.5 %gather_fusion.2 = bf16[16,80,128]{2,1,0:T(8,128)(2,1)S(1)} fusion(bf16[320,80,128]{2,1,0:T(8,128)(2,1)} %constant_dynamic-update-slice_fusion, s32[1024]{0:T(1024)S(1)} %get-tuple-element.28), kind=kCustom, calls=%fused_computation.2 | custom fusion | bytes 655424 | tf_op jit(solution)/shard_map/gather | solution.py:85
  53.9 3.5 %gather_fusion.1 = bf16[16,80,128]{2,1,0:T(8,128)(2,1)S(1)} fusion(bf16[320,80,128]{2,1,0:T(8,128)(2,1)} %constant_dynamic-update-slice_fusion, s32[1024]{0:T(1024)S(1)} %get-tuple-element.29), kind=kCustom, calls=%fused_computation.1 | custom fusion | bytes 655424 | tf_op jit(solution)/shard_map/gather | solution.py:85
  57.3 3.5 %gather_fusion = bf16[16,80,128]{2,1,0:T(8,128)(2,1)S(1)} fusion(bf16[320,80,128]{2,1,0:T(8,128)(2,1)} %constant_dynamic-update-slice_fusion, s32[1024]{0:T(1024)S(1)} %get-tuple-element.30), kind=kCustom, calls=%fused_computation | custom fusion | bytes 655424 | tf_op jit(solution)/shard_map/gather | solution.py:85
  60.8 0.0 copy-done
  60.8 0.6 fusion.1
  61.4 0.4 convolution_bitcast_fusion.7
  61.8 0.4 convolution_bitcast_fusion.6
  62.2 0.4 convolution_bitcast_fusion.5
  62.6 0.4 convolution_bitcast_fusion.4
  63.0 0.4 convolution_bitcast_fusion.3
  63.4 0.4 convolution_bitcast_fusion.2
  63.9 0.4 convolution_bitcast_fusion.1
  64.3 0.4 convolution_bitcast_fusion
  64.8 0.8 copy.14
  65.6 5.5 %all-to-all-start.1 = ((bf16[8,8,10,80]{3,1,2,0:T(8,128)(2,1)}), bf16[8,8,10,80]{3,1,2,0:T(8,128)(2,1)S(1)}, u32[]{:S(2)}, u32[]{:S(2)}) async-start(bf16[8,8,10,80]{3,1,2,0:T(8,128)(2,1)} %copy.14), calls=%async_computation.1 | async-start | bytes 327680 | tf_op jit(solution)/shard_map/all_to_all | solution.py:34
  71.1 1.7 %copy.12 = bf16[80,256,16]{0,2,1:T(8,128)(2,1)} copy(bf16[80,256,16]{1,0,2:T(8,128)(2,1)S(1)} %fusion.1) | data formatting | bytes 1310720 | tf_op jit(solution)/shard_map/convert_element_type | solution.py:92
  72.9 3.8 %all-to-all-done.1 = bf16[8,8,10,80]{3,1,2,0:T(8,128)(2,1)S(1)} async-done(((bf16[8,8,10,80]{3,1,2,0:T(8,128)(2,1)}), bf16[8,8,10,80]{3,1,2,0:T(8,128)(2,1)S(1)}, u32[]{:S(2)}, u32[]{:S(2)}) %all-to-all-start.1) | async-done | bytes 102432 | tf_op jit(solution)/shard_map/all_to_all | solution.py:34
  76.7 4.4 %all-to-all-start = ((bf16[80,256,16]{0,2,1:T(8,128)(2,1)}), bf16[80,256,16]{0,2,1:T(8,128)(2,1)S(1)}, u32[]{:S(2)}, u32[]{:S(2)}) async-start(bf16[80,256,16]{0,2,1:T(8,128)(2,1)} %copy.12), calls=%async_computation | async-start | bytes 2097152 | tf_op jit(solution)/shard_map/all_to_all | solution.py:96
  81.1 0.7 convert_reduce_fusion
  81.7 14.3 %all-to-all-done = bf16[80,256,16]{0,2,1:T(8,128)(2,1)S(1)} async-done(((bf16[80,256,16]{0,2,1:T(8,128)(2,1)}), bf16[80,256,16]{0,2,1:T(8,128)(2,1)S(1)}, u32[]{:S(2)}, u32[]{:S(2)}) %all-to-all-start) | async-done | bytes 655392 | tf_op jit(solution)/shard_map/all_to_all | solution.py:96
  96.1 0.3 copy.13
  96.4 1.4 %copy.16 = bf16[80,32,128]{2,1,0:T(8,128)(2,1)} copy(bf16[80,32,128]{0,2,1:T(8,128)(2,1)S(1)} %bitcast.68) | data formatting | bytes 1310720
  (27 shorter events, 0.2 us)
Async XLA Ops:
  0.6 60.2 %copy-start = (bf16[16,256,128]{2,1,0:T(8,128)(2,1)S(1)}, bf16[16,256,128]{2,1,0:T(8,128)(2,1)}, u32[]{:S(2)}) copy-start(bf16[16,256,128]{2,1,0:T(8,128)(2,1)} %param.7) | copy-start | bytes 3145732
  0.6 25.7 %copy-start.2 = (f32[128,4]{0,1:T(4,128)S(1)}, f32[128,4]{0,1:T(4,128)}, u32[]{:S(2)}) copy-start(f32[128,4]{0,1:T(4,128)} %param.9) | copy-start | bytes 6148
  0.7 25.8 %copy-start.3 = (s32[128,4]{0,1:T(4,128)S(1)}, s32[128,4]{0,1:T(4,128)}, u32[]{:S(2)}) copy-start(s32[128,4]{0,1:T(4,128)} %param.8) | copy-start | bytes 6148
  0.7 26.0 %copy-start.1 = (bf16[256,16]{0,1:T(8,128)(2,1)S(1)}, bf16[256,16]{0,1:T(8,128)(2,1)}, u32[]{:S(2)}) copy-start(bf16[256,16]{0,1:T(8,128)(2,1)} %param.11) | copy-start | bytes 24580
  2.1 36.2 %collective-permute-start = (bf16[32,80,128]{2,1,0:T(8,128)(2,1)S(1)}, bf16[32,80,128]{2,1,0:T(8,128)(2,1)}, u32[]{:S(2)}, u32[]{:S(2)}) collective-permute-start(bf16[32,80,128]{2,1,0:T(8,128)(2,1)S(1)} %get-tuple-element.10), channel_id=1, source_target_pairs={{0,8},{8,16},{16,24},{24,32},{32,40},{40,48},{48,56},{56,64},{64,7... | collective-permute-start | bytes 1966088 | tf_op jit(solution)/shard_map/ppermute | solution.py:18
  6.2 39.9 %collective-permute-start.1 = (bf16[32,80,128]{2,1,0:T(8,128)(2,1)S(1)}, bf16[32,80,128]{2,1,0:T(8,128)(2,1)S(1)}, u32[]{:S(2)}, u32[]{:S(2)}) collective-permute-start(bf16[32,80,128]{2,1,0:T(8,128)(2,1)S(1)} %get-tuple-element.9), channel_id=1, source_target_pairs={{8,0},{16,8},{24,16},{32,24},{40,32},{48,40},{56,48},{64,56},{72,6... | collective-permute-start | bytes 1966088 | tf_op jit(solution)/shard_map/ppermute | solution.py:21
  65.6 11.1 %all-to-all-start.1 = ((bf16[8,8,10,80]{3,1,2,0:T(8,128)(2,1)}), bf16[8,8,10,80]{3,1,2,0:T(8,128)(2,1)S(1)}, u32[]{:S(2)}, u32[]{:S(2)}) async-start(bf16[8,8,10,80]{3,1,2,0:T(8,128)(2,1)} %copy.14), calls=%async_computation.1 | async-start | bytes 327680 | tf_op jit(solution)/shard_map/all_to_all | solution.py:34
  76.7 19.4 %all-to-all-start = ((bf16[80,256,16]{0,2,1:T(8,128)(2,1)}), bf16[80,256,16]{0,2,1:T(8,128)(2,1)S(1)}, u32[]{:S(2)}, u32[]{:S(2)}) async-start(bf16[80,256,16]{0,2,1:T(8,128)(2,1)} %copy.12), calls=%async_computation | async-start | bytes 2097152 | tf_op jit(solution)/shard_map/all_to_all | solution.py:96
where the time goes:
time: 98.3 us; the launch traced here: 97.7 us
  starting transfers between devices  33.5 us (34%)
  waiting for transfers between devices  29.7 us (30%)
  local copies, waits for them, and re-layouts  28.5 us (29%)
  matrix products  3.64 us (4%)
  between operations  1.63 us (2%)
    ppermute x1, starting transfers between devices, extended_2(): lax.ppermute(lax.slice_in_dim(block, 0, width, axis=dim), axis, backward)  19.6 us
    all_to_all x1, waiting for transfers between devices, shards(): lax.all_to_all(perturbed, 'chan', split_axis=1, concat_axis=2, tiled=True)  14.3 us
    gather x4, local copies, waits for them, and re-layouts, shards(): extended[own_offsets[:, column_slot]].astype(jnp.float32)  13.9 us
    ppermute x1, waiting for transfers between devices, extended_2(): lax.ppermute(lax.slice_in_dim(block, block.shape[dim] - width, None, axis...  11.5 us
    unnamed x18, local copies, waits for them, and re-layouts  9.14 us
    all_to_all x1, starting transfers between devices, sent_and_summed(): lax.all_to_all(pieces, axis, split_axis=0, concat_axis=0, tiled=True)  5.55 us
    all_to_all x1, starting transfers between devices, shards(): lax.all_to_all(perturbed, 'chan', split_axis=1, concat_axis=2, tiled=True)  4.37 us
    ppermute x1, starting transfers between devices, extended_2(): lax.ppermute(lax.slice_in_dim(block, block.shape[dim] - width, None, axis...  4.02 us
  transfers between devices with their start and end apart: 4, of which 3 were waited for; matrix products, arithmetic and copies ran while one was open for 11% of the time, Pallas kernels for 0%

commit v1 on v0

v1 whole, which is shorter than its diff:
```python
import jax
import jax.numpy as jnp
from jax import lax
from jax.experimental import pallas as pl
from jax.experimental.pallas import tpu as pltpu
from jax.sharding import PartitionSpec as P


CH = 256
OBS_DEV = 128
HALO = 32
PTS = 8
FP = 4
MIB = 1024 * 1024

VMEM = pltpu.MemorySpace.VMEM
SMEM = pltpu.MemorySpace.SMEM
NT = (((1,), (1,)), ((), ()))


def taper(distance, half_width):
    relative = jnp.abs(distance) / half_width
    near_part = (
        ((-0.25 * relative + 0.5) * relative + 0.625) * relative - 5.0 / 3.0
    ) * relative * relative + 1.0
    bounded = jnp.maximum(relative, 1.0)
    far_part = (
        ((((relative / 12.0 - 0.5) * relative + 0.625) * relative + 5.0 / 3.0) * relative - 5.0)
        * relative
        + 4.0
        - 2.0 / (3.0 * bounded)
    )
    return jnp.where(relative <= 1.0, near_part, jnp.where(relative <= 2.0, far_part, 0.0))


def home_mix(ints, gains, anomaly, n, tile_cols):
    total = None
    for f in range(FP):
        col = ints[f * OBS_DEV + n] - HALO
        inside = jnp.logical_and(col >= 0, col < tile_cols)
        gain = jnp.where(inside, gains[f * OBS_DEV + n], 0.0)
        term = gain * anomaly[jnp.clip(col, 0, tile_cols - 1)].astype(jnp.float32)
        total = term if total is None else total + term
    return total


def side_mix(ints, gains, halo, n, first):
    total = None
    for f in range(FP):
        col = ints[f * OBS_DEV + n] - first
        inside = jnp.logical_and(col >= 0, col < HALO)
        gain = jnp.where(inside, gains[f * OBS_DEV + n], 0.0)
        term = gain * halo[jnp.clip(col, 0, HALO - 1)].astype(jnp.float32)
        total = term if total is None else total + term
    return total


def reaches(ints, n, tile_cols):
    cols = [ints[f * OBS_DEV + n] for f in range(FP)]
    least = jnp.minimum(jnp.minimum(cols[0], cols[1]), jnp.minimum(cols[2], cols[3]))
    most = jnp.maximum(jnp.maximum(cols[0], cols[1]), jnp.maximum(cols[2], cols[3]))
    return least < HALO, most >= HALO + tile_cols


def home_kernel(tile_cols, ints, gains, anomaly, whole, own):
    share = own.shape[0]
    first_obs = ints[FP * OBS_DEV]

    def each(n, carry):
        whole[n] = home_mix(ints, gains, anomaly, n, tile_cols).astype(whole.dtype)
        return carry

    lax.fori_loop(0, OBS_DEV, each, 0, unroll=4)

    def each_own(i, carry):
        own[i] = whole[first_obs + i]
        return carry

    lax.fori_loop(0, share, each_own, 0, unroll=4)


def add_halos(ints, gains, low, high, n, tile_cols, ref, i):
    to_low, to_high = reaches(ints, n, tile_cols)

    @pl.when(to_low)
    def _():
        ref[i] = (ref[i].astype(jnp.float32) + side_mix(ints, gains, low, n, 0)).astype(ref.dtype)

    @pl.when(to_high)
    def _():
        ref[i] = (
            ref[i].astype(jnp.float32) + side_mix(ints, gains, high, n, HALO + tile_cols)
        ).astype(ref.dtype)


def gram_kernel(tile_cols, ints, gains, low, high, own, jac, weight, gram, mixed, products, turned):
    share = own.shape[0]
    members = own.shape[1]
    first_obs = ints[FP * OBS_DEV]
    live_count = ints[FP * OBS_DEV + 1]
    mixed[...] = own[...]

    def each(i, carry):
        add_halos(ints, gains, low, high, first_obs + i, tile_cols, mixed, i)
        return carry

    lax.fori_loop(0, share, each, 0)
    for i in range(share):
        live = jnp.where(first_obs + i < live_count, 1.0, 0.0)
        radiance = lax.dot_general(mixed[i], jac[i], NT, preferred_element_type=jnp.float32)
        pert = (radiance * live).astype(jnp.bfloat16)
        scaled = (pert.astype(jnp.float32) * weight[i : i + 1, :].astype(jnp.float32)).astype(
            jnp.bfloat16
        )
        products[i] = lax.dot_general(scaled, pert, NT, preferred_element_type=jnp.float32)
    for p in range(PTS):
        total = None
        for i in range(share):
            term = gains[FP * OBS_DEV + p * share + i] * products[i]
            total = term if total is None else total + term
        turned[pl.ds(p, members, stride=PTS), 0:members] = total
    gram[...] = turned[:, 0:members].reshape(members, PTS, members).astype(gram.dtype)


def mix_kernel(tile_cols, ints, gains, low, high, home, after, mixed):
    def each(n, carry):
        mixed[n] = home[n]
        add_halos(ints, gains, low, high, n, tile_cols, mixed, n)
        return carry

    lax.fori_loop(0, OBS_DEV, each, 0)


def params(mib):
    return pltpu.CompilerParams(vmem_limit_bytes=mib * MIB)


def cost(flops, bytes_accessed):
    return pl.CostEstimate(flops=flops, bytes_accessed=bytes_accessed, transcendentals=0)


def specs(*spaces):
    return [pl.BlockSpec(memory_space=space) for space in spaces]


def shards(anomaly, jacobian, foot_cols, foot_weight, obs_count, obs_weight):
    col_groups = lax.axis_size("cols")
    chans = lax.axis_size("chan")
    tile_index = lax.axis_index("cols")
    chan_index = lax.axis_index("chan")
    tile_cols, members, levels = anomaly.shape
    obs_share = jacobian.shape[0]
    block = CH // chans

    forward = [(i, (i + 1) % col_groups) for i in range(col_groups)]
    backward = [(target, source) for source, target in forward]
    low = lax.ppermute(anomaly[tile_cols - HALO :], "cols", forward)
    high = lax.ppermute(anomaly[:HALO], "cols", backward)

    pieces = jacobian.reshape(obs_share, chans, block, levels).transpose(1, 0, 2, 3)
    jac_block = lax.all_to_all(pieces, "chan", split_axis=0, concat_axis=0, tiled=True)
    jac_block = jac_block.reshape(OBS_DEV, block, levels)

    first_obs = chan_index * obs_share
    columns = foot_cols.T
    column_gains = foot_weight.T
    offsets = jnp.mod(columns - tile_index * tile_cols + HALO, tile_cols * col_groups)
    centers = jnp.sum(column_gains * (offsets - HALO).astype(jnp.float32), axis=0) / jnp.sum(
        column_gains, axis=0
    )
    own_centers = lax.dynamic_slice_in_dim(centers, first_obs, obs_share, 0)
    spacing = tile_cols / PTS
    points = (jnp.arange(PTS, dtype=jnp.float32) + 0.5) * spacing
    locality = taper(own_centers[None, :] - points[:, None], spacing) / (CH * OBS_DEV)
    ints = jnp.concatenate(
        [offsets.reshape(-1), first_obs[None].astype(jnp.int32), obs_count.astype(jnp.int32)]
    )
    gains = jnp.concatenate([column_gains.reshape(-1), locality.reshape(-1)])

    tile = jax.ShapeDtypeStruct((OBS_DEV, members, levels), jnp.bfloat16)
    share = jax.ShapeDtypeStruct((obs_share, members, levels), jnp.bfloat16)
    home, own = pl.pallas_call(
        lambda *refs: home_kernel(tile_cols, *refs),
        out_shape=(tile, share),
        in_specs=specs(SMEM, SMEM, VMEM),
        out_specs=tuple(specs(VMEM, VMEM)),
        compiler_params=params(24),
        cost_estimate=cost(4_000_000_000, 8_000_000),
        name="home_mix",
    )(ints, gains, anomaly)

    gram = pl.pallas_call(
        lambda *refs: gram_kernel(tile_cols, *refs),
        out_shape=jax.ShapeDtypeStruct((members, PTS, members), jnp.bfloat16),
        in_specs=specs(SMEM, SMEM, VMEM, VMEM, VMEM, VMEM, VMEM),
        out_specs=pl.BlockSpec(memory_space=VMEM),
        scratch_shapes=[
            pltpu.VMEM((obs_share, members, levels), jnp.bfloat16),
            pltpu.VMEM((obs_share, members, members), jnp.float32),
            pltpu.VMEM((members * PTS, 128), jnp.float32),
        ],
        compiler_params=params(16),
        cost_estimate=cost(2_000_000_000, 3_000_000),
        name="gram",
    )(ints, gains, low, high, own, jacobian, obs_weight.T)
    arrived = lax.all_to_all(gram, "chan", split_axis=0, concat_axis=0, tiled=True)

    mixed = pl.pallas_call(
        lambda *refs: mix_kernel(tile_cols, *refs),
        out_shape=tile,
        in_specs=specs(SMEM, SMEM, VMEM, VMEM, VMEM, pl.ANY),
        out_specs=pl.BlockSpec(memory_space=VMEM),
        compiler_params=params(16),
        cost_estimate=cost(2_000_000_000, 6_000_000),
        name="tile_mix",
    )(ints, gains, low, high, home, gram)
    radiance = jnp.einsum("ncl,nml->mcn", jac_block, mixed, preferred_element_type=jnp.float32)
    live_mask = (jnp.arange(OBS_DEV, dtype=jnp.int32) < obs_count[0]).astype(jnp.float32)
    perturbed = (radiance * live_mask[None, None, :]).astype(jnp.bfloat16)

    gram_rows = arrived.reshape(chans, members // chans, PTS, members).astype(jnp.float32).sum(0)
    return perturbed, gram_rows.transpose(1, 0, 2)


def solution(mesh):
    return jax.shard_map(
        shards,
        mesh=mesh,
        in_specs=(
            P("cols", None, None),
            P(("cols", "chan"), None, None),
            P("cols", None),
            P("cols", None),
            P("cols"),
            P(None, ("cols", "chan")),
        ),
        out_specs=(P(None, "chan", "cols"), P("cols", "chan", None)),
        check_vma=False,
    )
```

time: 98.3 us -> 83.8 us (0.85)
  local copies, waits for them, and re-layouts: 28.5 us -> 13.7 us
  waiting for transfers between devices: 29.7 us -> 16.8 us
  Pallas kernels: 0 us -> 12.4 us
    gather x4 -> x0, local copies, waits for them, and re-layouts: 13.9 us -> none  [shards(): extended[own_offsets[:, column_slot]].astype(jnp.float32)]
    pallas_call x0 -> x3, Pallas kernels: none -> 12.4 us  [the longest x1 4.76 us: shards(): pl.pallas_call(lambda *refs: gram_kernel(tile_cols, *refs), out_shape=jax...]
    all_to_all x2, waiting for transfers between devices: 18.2 us -> 11.5 us  [the longest x1 7.07 us: shards(): lax.all_to_all(pieces, 'chan', split_axis=0, concat_axis=0, tiled=True)]
    ppermute x2, waiting for transfers between devices: 11.5 us -> 5.27 us  [the longest x1 4.26 us: shards(): low = lax.ppermute(anomaly[tile_cols - HALO:], 'cols', forward)]
    convert_element_type x1 -> x0, local copies, waits for them, and re-layouts: 1.72 us -> none  [shards(): perturbed = (radiance * live_mask[None, None, :]).astype(jnp.bfloat16)]
    reshape x0 -> x1, local copies, waits for them, and re-layouts: none -> 1.1 us  [shards(): jacobian.reshape(obs_share, chans, block, levels).transpose(1, 0, 2, 3)]
    slice x1, local copies, waits for them, and re-layouts: 1.45 us -> 2.44 us  [shards(): high = lax.ppermute(anomaly[:HALO], 'cols', backward)]
    unnamed x18 -> x19, local copies, waits for them, and re-layouts: 9.14 us -> 9.8 us
  transfers between devices with their start and end apart: 4 -> 4, of which waited for: 3 -> 4; matrix products, arithmetic and copies ran while one was open for 11% -> 3% of each run, Pallas kernels for 0% -> 9%
where the time goes in v1:
time: 83.8 us; the launch traced here: 83.3 us
  starting transfers between devices  34.4 us (41%)
  waiting for transfers between devices  16.8 us (20%)
  local copies, waits for them, and re-layouts  13.7 us (16%)
  Pallas kernels  12.4 us (15%)
  matrix products  3.67 us (4%)
  between operations  1.42 us (2%)
  other arithmetic  0.92 us (1%)
    ppermute x1, starting transfers between devices, shards(): high = lax.ppermute(anomaly[:HALO], 'cols', backward)  19.6 us
    unnamed x19, local copies, waits for them, and re-layouts  9.8 us
    all_to_all x1, waiting for transfers between devices, shards(): lax.all_to_all(pieces, 'chan', split_axis=0, concat_axis=0, tiled=True)  7.07 us
    all_to_all x1, starting transfers between devices, shards(): lax.all_to_all(gram, 'chan', split_axis=0, concat_axis=0, tiled=True)  5.82 us
    all_to_all x1, starting transfers between devices, shards(): lax.all_to_all(pieces, 'chan', split_axis=0, concat_axis=0, tiled=True)  5.04 us
    pallas_call x1, Pallas kernels, shards(): pl.pallas_call(lambda *refs: gram_kernel(tile_cols, *refs), out_shape=jax...  4.76 us
    pallas_call x1, Pallas kernels, shards(): pl.pallas_call(lambda *refs: mix_kernel(tile_cols, *refs), out_shape=tile...  4.54 us
    all_to_all x1, waiting for transfers between devices, shards(): lax.all_to_all(gram, 'chan', split_axis=0, concat_axis=0, tiled=True)  4.45 us
  transfers between devices with their start and end apart: 4, of which 4 were waited for; matrix products, arithmetic and copies ran while one was open for 3% of the time, Pallas kernels for 9%

profile of v1, /device:TPU:1, one launch (start us, length us, event | category | flops | bytes accessed | tf_op | source)
XLA Modules:
  0.0 83.3 jit_solution(8012453429627429683)
XLA Ops:
  0.6 0.0 copy-start.7
  0.6 0.0 copy-start.8
  0.6 2.4 %fusion.7 = (bf16[32,80,128]{2,1,0:T(8,128)(2,1)}, bf16[32,80,128]{2,1,0:T(8,128)(2,1)}) fusion(bf16[256,80,128]{2,1,0:T(8,128)(2,1)} %refs_2_.1), kind=kLoop, calls=%fused_computation.25 | loop fusion | bytes 2621440 | tf_op jit(solution)/shard_map/slice | solution.py:158
  3.1 4.0 %collective-permute-start = (bf16[32,80,128]{2,1,0:T(8,128)(2,1)}, bf16[32,80,128]{2,1,0:T(8,128)(2,1)S(1)}, u32[]{:S(2)}, u32[]{:S(2)}) collective-permute-start(bf16[32,80,128]{2,1,0:T(8,128)(2,1)} %get-tuple-element.9), channel_id=1, source_target_pairs={{0,8},{8,16},{16,24},{24,32},{32,40},{40,48},{48,56},{56,64},{64,7... | collective-permute-start | bytes 1966088 | tf_op jit(solution)/shard_map/ppermute | solution.py:157
  7.1 19.6 %collective-permute-start.1 = (bf16[32,80,128]{2,1,0:T(8,128)(2,1)}, bf16[32,80,128]{2,1,0:T(8,128)(2,1)S(1)}, u32[]{:S(2)}, u32[]{:S(2)}) collective-permute-start(bf16[32,80,128]{2,1,0:T(8,128)(2,1)} %get-tuple-element.8), channel_id=1, source_target_pairs={{8,0},{16,8},{24,16},{32,24},{40,32},{48,40},{56,48},{64,56},{72,6... | collective-permute-start | bytes 1966088 | tf_op jit(solution)/shard_map/ppermute | solution.py:158
  26.7 0.0 copy-done.7
  26.7 0.0 copy-done.8
  26.8 0.1 dynamic_slice.3
  26.9 0.1 multiply_add_fusion.1
  26.9 0.1 add.66
  27.0 0.1 div.30
  27.1 0.1 sub.49
  27.9 0.1 pad_add_fusion.refs_0_
  28.0 0.0 copy-start.1
  28.0 2.5 %copy-done.1 = bf16[256,80,128]{2,1,0:T(8,128)(2,1)S(1)} copy-done((bf16[256,80,128]{2,1,0:T(8,128)(2,1)S(1)}, bf16[256,80,128]{2,1,0:T(8,128)(2,1)}, u32[]{:S(2)}) %copy-start.1) | copy-done | bytes 5242904
  30.5 0.0 copy-start
  30.5 0.0 copy-start.4
  30.5 3.1 %home_mix.1 = (bf16[128,80,128]{2,1,0:T(8,128)(2,1)S(1)}, bf16[16,80,128]{2,1,0:T(8,128)(2,1)S(1)}) custom-call(s32[514]{0:T(1024)S(1)} %pad_add_fusion.refs_0_, f32[640]{0:T(1024)S(1)} %pad_maximum_fusion.refs_1_, bf16[256,80,128]{2,1,0:T(8,128)(2,1)S(1)} %copy-done.1), custom_call_target="tpu_custom_call" | custom-call | flops 4000000000 | bytes 8000000 | tf_op jit(solution)/shard_map/home_mix/pallas_call | solution.py:182
  33.6 0.0 copy-start.5
  33.6 1.5 %copy-done.5 = bf16[128,80,128]{2,1,0:T(8,128)(2,1)} copy-done((bf16[128,80,128]{2,1,0:T(8,128)(2,1)}, bf16[128,80,128]{2,1,0:T(8,128)(2,1)S(1)}, u32[]{:S(2)}) %copy-start.5) | copy-done | bytes 2621464
  35.1 4.3 %collective-permute-done.refs_2_ = bf16[32,80,128]{2,1,0:T(8,128)(2,1)S(1)} collective-permute-done((bf16[32,80,128]{2,1,0:T(8,128)(2,1)}, bf16[32,80,128]{2,1,0:T(8,128)(2,1)S(1)}, u32[]{:S(2)}, u32[]{:S(2)}) %collective-permute-start) | collective-permute-done | bytes 655392 | tf_op jit(solution)/shard_map/ppermute | solution.py:157
  39.4 1.0 %collective-permute-done.1.refs_3_ = bf16[32,80,128]{2,1,0:T(8,128)(2,1)S(1)} collective-permute-done((bf16[32,80,128]{2,1,0:T(8,128)(2,1)}, bf16[32,80,128]{2,1,0:T(8,128)(2,1)S(1)}, u32[]{:S(2)}, u32[]{:S(2)}) %collective-permute-start.1) | collective-permute-done | bytes 655392 | tf_op jit(solution)/shard_map/ppermute | solution.py:158
  40.4 0.0 copy-start.2
  40.4 0.0 copy-done
  40.4 0.0 copy-done.4
  40.4 4.8 %gram.1.refs_5_ = bf16[80,8,80]{2,1,0:T(8,128)(2,1)} custom-call(s32[514]{0:T(1024)S(1)} %pad_add_fusion.refs_0_, f32[640]{0:T(1024)S(1)} %pad_maximum_fusion.refs_1_, bf16[32,80,128]{2,1,0:T(8,128)(2,1)S(1)} %collective-permute-done.refs_2_, bf16[32,80,128]{2,1,0:T(8,128)(2,1)S(1)} %collective-permute-done.1.refs_3_, ...), custom_call_target="tpu_custom_call" | custom-call | flops 2000000000 | bytes 3000000 | tf_op jit(solution)/shard_map/gram/pallas_call | solution.py:192
  45.2 0.0 copy-done.2
  45.2 5.8 %all-to-all-start.1 = ((bf16[80,8,80]{2,1,0:T(8,128)(2,1)}), bf16[80,8,80]{2,1,0:T(8,128)(2,1)S(1)}, u32[]{:S(2)}, u32[]{:S(2)}) async-start(bf16[80,8,80]{2,1,0:T(8,128)(2,1)} %gram.1.refs_5_), calls=%async_computation.1 | async-start | bytes 327680 | tf_op jit(solution)/shard_map/all_to_all | solution.py:206
  51.0 1.1 %copy.11 = bf16[16,8,32,128]{3,2,0,1:T(8,128)(2,1)} copy(bf16[16,8,32,128]{3,2,1,0:T(8,128)(2,1)S(1)} %bitcast.32) | data formatting | bytes 2097152 | tf_op jit(solution)/shard_map/reshape | solution.py:160
  52.1 4.4 %all-to-all-done.1 = bf16[80,8,80]{2,1,0:T(8,128)(2,1)S(1)} async-done(((bf16[80,8,80]{2,1,0:T(8,128)(2,1)}), bf16[80,8,80]{2,1,0:T(8,128)(2,1)S(1)}, u32[]{:S(2)}, u32[]{:S(2)}) %all-to-all-start.1) | async-done | bytes 102432 | tf_op jit(solution)/shard_map/all_to_all | solution.py:206
  56.5 5.0 %all-to-all-start = ((bf16[8,16,32,128]{3,2,1,0:T(8,128)(2,1)}), bf16[8,16,32,128]{3,2,1,0:T(8,128)(2,1)}, u32[]{:S(2)}, u32[]{:S(2)}) async-start(bf16[8,16,32,128]{3,2,1,0:T(8,128)(2,1)} %bitcast.30), calls=%async_computation | async-start | bytes 2097152 | tf_op jit(solution)/shard_map/all_to_all | solution.py:161
  61.6 0.0 copy-start.3
  61.6 1.1 %copy-done.3 = bf16[32,80,128]{2,1,0:T(8,128)(2,1)S(1)} copy-done((bf16[32,80,128]{2,1,0:T(8,128)(2,1)S(1)}, bf16[32,80,128]{2,1,0:T(8,128)(2,1)}, u32[]{:S(2)}) %copy-start.3) | copy-done | bytes 655384
  62.7 0.0 copy-start.6
  62.7 1.7 %copy-done.6 = bf16[128,80,128]{2,1,0:T(8,128)(2,1)S(1)} copy-done((bf16[128,80,128]{2,1,0:T(8,128)(2,1)S(1)}, bf16[128,80,128]{2,1,0:T(8,128)(2,1)}, u32[]{:S(2)}) %copy-start.6) | copy-done | bytes 2621464
  64.4 4.5 %tile_mix.1 = bf16[128,80,128]{2,1,0:T(8,128)(2,1)S(1)} custom-call(s32[514]{0:T(1024)S(1)} %pad_add_fusion.refs_0_, f32[640]{0:T(1024)S(1)} %pad_maximum_fusion.refs_1_, bf16[32,80,128]{2,1,0:T(8,128)(2,1)S(1)} %collective-permute-done.refs_2_, bf16[32,80,128]{2,1,0:T(8,128)(2,1)S(1)} %copy-done.3, bf16[128,80,128]{2,1,0:T(8,128)(2,1)S(1)} %copy-done.6, ...), custom_call_target="tpu_custom_call" | custom-call | flops 2000000000 | bytes 6000000 | tf_op jit(solution)/shard_map/tile_mix/pallas_call | solution.py:208
  69.0 0.7 convert_reduce_fusion
  69.6 7.1 %all-to-all-done = bf16[8,16,32,128]{3,2,1,0:T(8,128)(2,1)} async-done(((bf16[8,16,32,128]{3,2,1,0:T(8,128)(2,1)}), bf16[8,16,32,128]{3,2,1,0:T(8,128)(2,1)}, u32[]{:S(2)}, u32[]{:S(2)}) %all-to-all-start) | async-done | bytes 1048608 | tf_op jit(solution)/shard_map/all_to_all | solution.py:161
  76.7 3.7 %fusion = bf16[80,32,128]{0,1,2:T(8,128)(2,1)} fusion(bf16[128,80,128]{2,1,0:T(8,128)(2,1)S(1)} %tile_mix.1, bf16[128,32,128]{2,1,0:T(8,128)(2,1)} %bitcast.8, f32[128]{0:T(128)S(1)} %compare_convert_fusion), kind=kOutput, calls=%fused_computation.1 | convolution fusion | flops 84541440 | bytes 4325888 | tf_op jit(solution)/shard_map/ncl,nml->mcn/dot_general | solution.py:217
  80.3 3.0 %copy.9 = bf16[80,32,128]{2,1,0:T(8,128)(2,1)} copy(bf16[80,32,128]{0,1,2:T(8,128)(2,1)} %fusion) | data formatting | bytes 1310720
  (8 shorter events, 0.1 us)
Async XLA Ops:
  0.6 26.1 %copy-start.7 = (f32[128,4]{0,1:T(4,128)S(1)}, f32[128,4]{0,1:T(4,128)}, u32[]{:S(2)}) copy-start(f32[128,4]{0,1:T(4,128)} %param.9) | copy-start | bytes 6148
  0.6 26.1 %copy-start.8 = (s32[128,4]{0,1:T(4,128)S(1)}, s32[128,4]{0,1:T(4,128)}, u32[]{:S(2)}) copy-start(s32[128,4]{0,1:T(4,128)} %param.8) | copy-start | bytes 6148
  3.1 36.3 %collective-permute-start = (bf16[32,80,128]{2,1,0:T(8,128)(2,1)}, bf16[32,80,128]{2,1,0:T(8,128)(2,1)S(1)}, u32[]{:S(2)}, u32[]{:S(2)}) collective-permute-start(bf16[32,80,128]{2,1,0:T(8,128)(2,1)} %get-tuple-element.9), channel_id=1, source_target_pairs={{0,8},{8,16},{16,24},{24,32},{32,40},{40,48},{48,56},{56,64},{64,7... | collective-permute-start | bytes 1966088 | tf_op jit(solution)/shard_map/ppermute | solution.py:157
  7.1 33.3 %collective-permute-start.1 = (bf16[32,80,128]{2,1,0:T(8,128)(2,1)}, bf16[32,80,128]{2,1,0:T(8,128)(2,1)S(1)}, u32[]{:S(2)}, u32[]{:S(2)}) collective-permute-start(bf16[32,80,128]{2,1,0:T(8,128)(2,1)} %get-tuple-element.8), channel_id=1, source_target_pairs={{8,0},{16,8},{24,16},{32,24},{40,32},{48,40},{56,48},{64,56},{72,6... | collective-permute-start | bytes 1966088 | tf_op jit(solution)/shard_map/ppermute | solution.py:158
  28.0 2.5 %copy-start.1 = (bf16[256,80,128]{2,1,0:T(8,128)(2,1)S(1)}, bf16[256,80,128]{2,1,0:T(8,128)(2,1)}, u32[]{:S(2)}) copy-start(bf16[256,80,128]{2,1,0:T(8,128)(2,1)} %refs_2_.1) | copy-start | bytes 15728644
  30.5 9.9 %copy-start = (bf16[16,256,128]{2,1,0:T(8,128)(2,1)S(1)}, bf16[16,256,128]{2,1,0:T(8,128)(2,1)}, u32[]{:S(2)}) copy-start(bf16[16,256,128]{2,1,0:T(8,128)(2,1)} %refs_5_.1) | copy-start | bytes 3145732
  30.5 9.9 %copy-start.4 = (bf16[256,16]{0,1:T(8,128)(2,1)S(1)}, bf16[256,16]{0,1:T(8,128)(2,1)}, u32[]{:S(2)}) copy-start(bf16[256,16]{0,1:T(8,128)(2,1)} %param.11) | copy-start | bytes 24580
  33.6 1.5 %copy-start.5 = (bf16[128,80,128]{2,1,0:T(8,128)(2,1)}, bf16[128,80,128]{2,1,0:T(8,128)(2,1)S(1)}, u32[]{:S(2)}) copy-start(bf16[128,80,128]{2,1,0:T(8,128)(2,1)S(1)} %get-tuple-element.4.refs_4_) | copy-start | bytes 7864324
  40.4 4.8 %copy-start.2 = (bf16[32,80,128]{2,1,0:T(8,128)(2,1)}, bf16[32,80,128]{2,1,0:T(8,128)(2,1)S(1)}, u32[]{:S(2)}) copy-start(bf16[32,80,128]{2,1,0:T(8,128)(2,1)S(1)} %collective-permute-done.1.refs_3_) | copy-start | bytes 1966084
  45.2 11.4 %all-to-all-start.1 = ((bf16[80,8,80]{2,1,0:T(8,128)(2,1)}), bf16[80,8,80]{2,1,0:T(8,128)(2,1)S(1)}, u32[]{:S(2)}, u32[]{:S(2)}) async-start(bf16[80,8,80]{2,1,0:T(8,128)(2,1)} %gram.1.refs_5_), calls=%async_computation.1 | async-start | bytes 327680 | tf_op jit(solution)/shard_map/all_to_all | solution.py:206
  56.5 20.1 %all-to-all-start = ((bf16[8,16,32,128]{3,2,1,0:T(8,128)(2,1)}), bf16[8,16,32,128]{3,2,1,0:T(8,128)(2,1)}, u32[]{:S(2)}, u32[]{:S(2)}) async-start(bf16[8,16,32,128]{3,2,1,0:T(8,128)(2,1)} %bitcast.30), calls=%async_computation | async-start | bytes 2097152 | tf_op jit(solution)/shard_map/all_to_all | solution.py:161
  61.6 1.1 %copy-start.3 = (bf16[32,80,128]{2,1,0:T(8,128)(2,1)S(1)}, bf16[32,80,128]{2,1,0:T(8,128)(2,1)}, u32[]{:S(2)}) copy-start(bf16[32,80,128]{2,1,0:T(8,128)(2,1)} %copy-done.2) | copy-start | bytes 1966084
  62.7 1.7 %copy-start.6 = (bf16[128,80,128]{2,1,0:T(8,128)(2,1)S(1)}, bf16[128,80,128]{2,1,0:T(8,128)(2,1)}, u32[]{:S(2)}) copy-start(bf16[128,80,128]{2,1,0:T(8,128)(2,1)} %copy-done.5) | copy-start | bytes 7864324

commit v2 on v1

--- a/solution.py
+++ b/solution.py
@@ -55,60 +55,60 @@
     return total
 
 
-def reaches(ints, n, tile_cols):
-    cols = [ints[f * OBS_DEV + n] for f in range(FP)]
-    least = jnp.minimum(jnp.minimum(cols[0], cols[1]), jnp.minimum(cols[2], cols[3]))
-    most = jnp.maximum(jnp.maximum(cols[0], cols[1]), jnp.maximum(cols[2], cols[3]))
-    return least < HALO, most >= HALO + tile_cols
-
-
-def home_kernel(tile_cols, ints, gains, anomaly, whole, own):
-    share = own.shape[0]
-    first_obs = ints[FP * OBS_DEV]
-
+def edge_kernel(anomaly, edge, sem):
+    core = lax.rem(lax.axis_index("chan"), 2)
+    first = jnp.where(core == 0, anomaly.shape[0] - HALO, 0)
+    copy = pltpu.make_async_copy(anomaly.at[pl.ds(first, HALO)], edge, sem)
+    copy.start()
+    copy.wait()
+
+
+def home_kernel(tile_cols, ints, gains, anomaly, home):
     def each(n, carry):
-        whole[n] = home_mix(ints, gains, anomaly, n, tile_cols).astype(whole.dtype)
+        home[n] = home_mix(ints, gains, anomaly, n, tile_cols).astype(home.dtype)
         return carry
 
     lax.fori_loop(0, OBS_DEV, each, 0, unroll=4)
 
-    def each_own(i, carry):
-        own[i] = whole[first_obs + i]
+
+def gram_kernel(tile_cols, ints, gains, ours, theirs, home, jac, weight, gram, mixed, perts, products, turned):
+    share, members = perts.shape[:2]
+    tail = (FP + 1) * OBS_DEV
+    first_obs = ints[tail]
+    live_count = ints[tail + 1]
+    first_ours = ints[tail + 2]
+    first_theirs = HALO + tile_cols - first_ours
+    mixed[...] = home[...]
+
+    def add(n, halo, first):
+        mixed[n] = (mixed[n].astype(jnp.float32) + side_mix(ints, gains, halo, n, first)).astype(
+            mixed.dtype
+        )
+
+    def each(n, carry):
+        reach = ints[FP * OBS_DEV + n]
+
+        @pl.when(reach > 0)
+        def _():
+            @pl.when(jnp.bitwise_and(reach, 1) > 0)
+            def _():
+                add(n, ours, first_ours)
+
+            @pl.when(jnp.bitwise_and(reach, 2) > 0)
+            def _():
+                add(n, theirs, first_theirs)
+
         return carry
 
-    lax.fori_loop(0, share, each_own, 0, unroll=4)
-
-
-def add_halos(ints, gains, low, high, n, tile_cols, ref, i):
-    to_low, to_high = reaches(ints, n, tile_cols)
-
-    @pl.when(to_low)
-    def _():
-        ref[i] = (ref[i].astype(jnp.float32) + side_mix(ints, gains, low, n, 0)).astype(ref.dtype)
-
-    @pl.when(to_high)
-    def _():
-        ref[i] = (
-            ref[i].astype(jnp.float32) + side_mix(ints, gains, high, n, HALO + tile_cols)
-        ).astype(ref.dtype)
-
-
-def gram_kernel(tile_cols, ints, gains, low, high, own, jac, weight, gram, mixed, products, turned):
-    share = own.shape[0]
-    members = own.shape[1]
-    first_obs = ints[FP * OBS_DEV]
-    live_count = ints[FP * OBS_DEV + 1]
-    mixed[...] = own[...]
-
-    def each(i, carry):
-        add_halos(ints, gains, low, high, first_obs + i, tile_cols, mixed, i)
-        return carry
-
-    lax.fori_loop(0, share, each, 0)
+    lax.fori_loop(0, OBS_DEV, each, 0, unroll=4)
     for i in range(share):
         live = jnp.where(first_obs + i < live_count, 1.0, 0.0)
-        radiance = lax.dot_general(mixed[i], jac[i], NT, preferred_element_type=jnp.float32)
-        pert = (radiance * live).astype(jnp.bfloat16)
+        radiance = lax.dot_general(
+            mixed[first_obs + i], jac[i], NT, preferred_element_type=jnp.float32
+        )
+        perts[i] = (radiance * live).astype(jnp.bfloat16)
+    for i in range(share):
+        pert = perts[i]
         scaled = (pert.astype(jnp.float32) * weight[i : i + 1, :].astype(jnp.float32)).astype(
             jnp.bfloat16
         )
@@ -122,15 +122,6 @@
     gram[...] = turned[:, 0:members].reshape(members, PTS, members).astype(gram.dtype)
 
 
-def mix_kernel(tile_cols, ints, gains, low, high, home, after, mixed):
-    def each(n, carry):
-        mixed[n] = home[n]
-        add_halos(ints, gains, low, high, n, tile_cols, mixed, n)
-        return carry
-
-    lax.fori_loop(0, OBS_DEV, each, 0)
-
-
 def params(mib):
     return pltpu.CompilerParams(vmem_limit_bytes=mib * MIB)
 
@@ -152,10 +143,24 @@
     obs_share = jacobian.shape[0]
     block = CH // chans
 
-    forward = [(i, (i + 1) % col_groups) for i in range(col_groups)]
-    backward = [(target, source) for source, target in forward]
-    low = lax.ppermute(anomaly[tile_cols - HALO :], "cols", forward)
-    high = lax.ppermute(anomaly[:HALO], "cols", backward)
+    core = lax.rem(chan_index, 2)
+    edge = pl.pallas_call(
+        edge_kernel,
+        out_shape=jax.ShapeDtypeStruct((HALO, members, levels), jnp.bfloat16),
+        in_specs=specs(pl.ANY),
+        out_specs=pl.BlockSpec(memory_space=VMEM),
+        scratch_shapes=[pltpu.SemaphoreType.DMA],
+        compiler_params=params(59),
+        cost_estimate=cost(1_000_000, 1_300_000),
+        name="edge",
+    )(anomaly)
+    to_side = [
+        (t * chans + j, (t + (1 if j % 2 == 0 else -1)) % col_groups * chans + j)
+        for t in range(col_groups)
+        for j in range(chans)
+    ]
+    ours = lax.ppermute(edge, ("cols", "chan"), to_side)
+    theirs = lax.ppermute(ours, "chan", [(j, j ^ 1) for j in range(chans)])
 
     pieces = jacobian.reshape(obs_share, chans, block, levels).transpose(1, 0, 2, 3)
     jac_block = lax.all_to_all(pieces, "chan", split_axis=0, concat_axis=0, tiled=True)
@@ -172,48 +177,42 @@
     spacing = tile_cols / PTS
     points = (jnp.arange(PTS, dtype=jnp.float32) + 0.5) * spacing
     locality = taper(own_centers[None, :] - points[:, None], spacing) / (CH * OBS_DEV)
-    ints = jnp.concatenate(
-        [offsets.reshape(-1), first_obs[None].astype(jnp.int32), obs_count.astype(jnp.int32)]
-    )
+    first_ours = jnp.where(core == 0, 0, HALO + tile_cols)
+    low_reach = jnp.min(offsets, axis=0) < HALO
+    high_reach = jnp.max(offsets, axis=0) >= HALO + tile_cols
+    ours_reach = jnp.where(core == 0, low_reach, high_reach)
+    theirs_reach = jnp.where(core == 0, high_reach, low_reach)
+    reach = ours_reach.astype(jnp.int32) + 2 * theirs_reach.astype(jnp.int32)
+    tail = jnp.stack([first_obs, obs_count[0], first_ours]).astype(jnp.int32)
+    ints = jnp.concatenate([offsets.reshape(-1), reach, tail])
     gains = jnp.concatenate([column_gains.reshape(-1), locality.reshape(-1)])
 
     tile = jax.ShapeDtypeStruct((OBS_DEV, members, levels), jnp.bfloat16)
-    share = jax.ShapeDtypeStruct((obs_share, members, levels), jnp.bfloat16)
-    home, own = pl.pallas_call(
+    home = pl.pallas_call(
         lambda *refs: home_kernel(tile_cols, *refs),
-        out_shape=(tile, share),
+        out_shape=tile,
         in_specs=specs(SMEM, SMEM, VMEM),
-        out_specs=tuple(specs(VMEM, VMEM)),
-        compiler_params=params(24),
+        out_specs=pl.BlockSpec(memory_space=VMEM),
+        compiler_params=params(12),
         cost_estimate=cost(4_000_000_000, 8_000_000),
         name="home_mix",
     )(ints, gains, anomaly)
 
-    gram = pl.pallas_call(
+    gram, mixed = pl.pallas_call(
         lambda *refs: gram_kernel(tile_cols, *refs),
-        out_shape=jax.ShapeDtypeStruct((members, PTS, members), jnp.bfloat16),
+        out_shape=(jax.ShapeDtypeStruct((members, PTS, members), jnp.bfloat16), tile),
         in_specs=specs(SMEM, SMEM, VMEM, VMEM, VMEM, VMEM, VMEM),
-        out_specs=pl.BlockSpec(memory_space=VMEM),
+        out_specs=tuple(specs(VMEM, VMEM)),
         scratch_shapes=[
-            pltpu.VMEM((obs_share, members, levels), jnp.bfloat16),
+            pltpu.VMEM((obs_share, members, CH), jnp.bfloat16),
             pltpu.VMEM((obs_share, members, members), jnp.float32),
             pltpu.VMEM((members * PTS, 128), jnp.float32),
         ],
         compiler_params=params(16),
-        cost_estimate=cost(2_000_000_000, 3_000_000),
+        cost_estimate=cost(6_000_000_000, 3_000_000),
         name="gram",
-    )(ints, gains, low, high, own, jacobian, obs_weight.T)
+    )(ints, gains, ours, theirs, home, jacobian, obs_weight.T)
     arrived = lax.all_to_all(gram, "chan", split_axis=0, concat_axis=0, tiled=True)
-
-    mixed = pl.pallas_call(
-        lambda *refs: mix_kernel(tile_cols, *refs),
-        out_shape=tile,
-        in_specs=specs(SMEM, SMEM, VMEM, VMEM, VMEM, pl.ANY),
-        out_specs=pl.BlockSpec(memory_space=VMEM),
-        compiler_params=params(16),
-        cost_estimate=cost(2_000_000_000, 6_000_000),
-        name="tile_mix",
-    )(ints, gains, low, high, home, gram)
     radiance = jnp.einsum("ncl,nml->mcn", jac_block, mixed, preferred_element_type=jnp.float32)
     live_mask = (jnp.arange(OBS_DEV, dtype=jnp.int32) < obs_count[0]).astype(jnp.float32)
     perturbed = (radiance * live_mask[None, None, :]).astype(jnp.bfloat16)

time: 83.8 us -> 58.5 us (0.70)
  waiting for transfers between devices: 16.8 us -> 1.01 us
  local copies, waits for them, and re-layouts: 13.7 us -> 7.01 us
  Pallas kernels: 12.4 us -> 9.74 us
    all_to_all x1, waiting for transfers between devices: 7.07 us -> 0.01 us  [shards(): lax.all_to_all(pieces, 'chan', split_axis=0, concat_axis=0, tiled=True)]
    all_to_all x1, waiting for transfers between devices: 4.45 us -> 0.01 us  [shards(): lax.all_to_all(gram, 'chan', split_axis=0, concat_axis=0, tiled=True)]
    unnamed x19 -> x13, local copies, waits for them, and re-layouts: 9.8 us -> 5.48 us
    ppermute x2, waiting for transfers between devices: 5.27 us -> 1.01 us  [the longest x1 1.01 us: shards(): ours = lax.ppermute(edge, ('cols', 'chan'), to_side)]
    pallas_call x3, Pallas kernels: 12.4 us -> 9.74 us  [the longest x1 4.6 us: shards(): pl.pallas_call(lambda *refs: gram_kernel(tile_cols, *refs), out_shape=(ja...]
    slice x1 -> x0, local copies, waits for them, and re-layouts: 2.44 us -> none  [shards(): high = lax.ppermute(anomaly[:HALO], 'cols', backward)]
    ppermute x2, starting transfers between devices: 23.6 us -> 25.5 us  [the longest x1 21.7 us: shards(): ours = lax.ppermute(edge, ('cols', 'chan'), to_side)]
    all_to_all x1, starting transfers between devices: 5.82 us -> 4.41 us  [shards(): lax.all_to_all(gram, 'chan', split_axis=0, concat_axis=0, tiled=True)]
  transfers between devices with their start and end apart: 4 -> 4, of which waited for: 4 -> 1; matrix products, arithmetic and copies ran while one was open for 3% -> 15% of each run, Pallas kernels for 9% -> 13%
where the time goes in v2:
time: 58.5 us; the launch traced here: 58.1 us
  starting transfers between devices  34.3 us (59%)
  Pallas kernels  9.74 us (17%)
  local copies, waits for them, and re-layouts  7.01 us (12%)
  matrix products  3.74 us (6%)
  between operations  1.43 us (2%)
  waiting for transfers between devices  1.01 us (2%)
  other arithmetic  0.86 us (1%)
    ppermute x1, starting transfers between devices, shards(): ours = lax.ppermute(edge, ('cols', 'chan'), to_side)  21.7 us
    unnamed x13, local copies, waits for them, and re-layouts  5.48 us
    pallas_call x1, Pallas kernels, shards(): pl.pallas_call(lambda *refs: gram_kernel(tile_cols, *refs), out_shape=(ja...  4.6 us
    all_to_all x1, starting transfers between devices, shards(): lax.all_to_all(gram, 'chan', split_axis=0, concat_axis=0, tiled=True)  4.41 us
    all_to_all x1, starting transfers between devices, shards(): lax.all_to_all(pieces, 'chan', split_axis=0, concat_axis=0, tiled=True)  4.41 us
    ppermute x1, starting transfers between devices, shards(): theirs = lax.ppermute(ours, 'chan', [(j, j ^ 1) for j in range(chans)])  3.79 us
    dot_general x1, matrix products, shards(): jnp.einsum('ncl,nml->mcn', jac_block, mixed, preferred_element_type=jnp.f...  3.74 us
    pallas_call x1, Pallas kernels, shards(): pl.pallas_call(lambda *refs: home_kernel(tile_cols, *refs), out_shape=til...  3.11 us
  transfers between devices with their start and end apart: 4, of which 1 were waited for; matrix products, arithmetic and copies ran while one was open for 15% of the time, Pallas kernels for 13%

profile of v2, /device:TPU:1, one launch (start us, length us, event | category | flops | bytes accessed | tf_op | source)
XLA Modules:
  0.0 58.1 jit_solution(8696780019520792749)
XLA Ops:
  0.6 0.0 copy-start.1
  0.6 2.0 %edge.1 = bf16[32,80,128]{2,1,0:T(8,128)(2,1)} custom-call(bf16[256,80,128]{2,1,0:T(8,128)(2,1)} %refs_2_.1), custom_call_target="tpu_custom_call" | custom-call | flops 1000000 | bytes 1300000 | tf_op jit(solution)/shard_map/edge/pallas_call | solution.py:147
  2.7 0.0 copy-start.4
  2.7 0.0 copy-start.5
  2.7 21.7 %collective-permute-start = (bf16[32,80,128]{2,1,0:T(8,128)(2,1)}, bf16[32,80,128]{2,1,0:T(8,128)(2,1)S(1)}, u32[]{:S(2)}, u32[]{:S(2)}) collective-permute-start(bf16[32,80,128]{2,1,0:T(8,128)(2,1)} %edge.1), channel_id=1, source_target_pairs={{0,8},{1,1017},{2,10},{3,1019},{4,12},{5,1021},{6,14},{7,1023},{8,... | collective-permute-start | bytes 1966088 | tf_op jit(solution)/shard_map/ppermute | solution.py:162
  24.4 0.0 copy-done.1
  24.4 1.1 %copy.11 = bf16[16,8,32,128]{3,2,0,1:T(8,128)(2,1)} copy(bf16[16,8,32,128]{3,2,1,0:T(8,128)(2,1)S(1)} %bitcast.29) | data formatting | bytes 2097152 | tf_op jit(solution)/shard_map/reshape | solution.py:165
  25.5 4.4 %all-to-all-start = ((bf16[8,16,32,128]{3,2,1,0:T(8,128)(2,1)}), bf16[8,16,32,128]{3,2,1,0:T(8,128)(2,1)}, u32[]{:S(2)}, u32[]{:S(2)}) async-start(bf16[8,16,32,128]{3,2,1,0:T(8,128)(2,1)} %bitcast.27), calls=%async_computation | async-start | bytes 2097152 | tf_op jit(solution)/shard_map/all_to_all | solution.py:166
  30.6 0.0 copy-done.4
  30.6 0.0 copy-done.5
  30.7 0.1 dynamic_slice.3
  30.7 0.1 multiply_add_fusion.1
  30.8 0.1 add.70
  30.9 0.1 div.30
  31.0 0.1 sub.49
  31.1 0.1 concatenate.6.refs_0_
  31.2 1.0 %collective-permute-done.refs_2_ = bf16[32,80,128]{2,1,0:T(8,128)(2,1)S(1)} collective-permute-done((bf16[32,80,128]{2,1,0:T(8,128)(2,1)}, bf16[32,80,128]{2,1,0:T(8,128)(2,1)S(1)}, u32[]{:S(2)}, u32[]{:S(2)}) %collective-permute-start) | collective-permute-done | bytes 655392 | tf_op jit(solution)/shard_map/ppermute | solution.py:162
  32.2 3.8 %collective-permute-start.1 = (bf16[32,80,128]{2,1,0:T(8,128)(2,1)S(1)}, bf16[32,80,128]{2,1,0:T(8,128)(2,1)S(1)}, u32[]{:S(2)}, u32[]{:S(2)}) collective-permute-start(bf16[32,80,128]{2,1,0:T(8,128)(2,1)S(1)} %collective-permute-done.refs_2_), channel_id=1, source_target_pairs={{0,1},{1,0},{2,3},{3,2},{4,5},{5,4},{6,7},{7,6},{8,9},{9,8},{10,11... | collective-permute-start | bytes 1966088 | tf_op jit(solution)/shard_map/ppermute | solution.py:163
  36.0 0.0 copy-start
  36.0 2.5 %copy-done = bf16[256,80,128]{2,1,0:T(8,128)(2,1)S(1)} copy-done((bf16[256,80,128]{2,1,0:T(8,128)(2,1)S(1)}, bf16[256,80,128]{2,1,0:T(8,128)(2,1)}, u32[]{:S(2)}) %copy-start) | copy-done | bytes 5242904
  38.5 0.0 copy-start.2
  38.5 0.0 copy-start.3
  38.5 3.1 %home_mix.1.refs_4_ = bf16[128,80,128]{2,1,0:T(8,128)(2,1)S(1)} custom-call(s32[643]{0:T(1024)S(1)} %concatenate.6.refs_0_, f32[640]{0:T(1024)S(1)} %pad_maximum_fusion.refs_1_, bf16[256,80,128]{2,1,0:T(8,128)(2,1)S(1)} %copy-done), custom_call_target="tpu_custom_call" | custom-call | flops 4000000000 | bytes 8000000 | tf_op jit(solution)/shard_map/home_mix/pallas_call | solution.py:191
  41.6 0.0 collective-permute-done.1.refs_3_
  41.7 0.0 copy-done.2
  41.7 0.0 copy-done.3
  41.7 4.6 %gram.1 = (bf16[80,8,80]{2,1,0:T(8,128)(2,1)}, bf16[128,80,128]{2,1,0:T(8,128)(2,1)S(1)}) custom-call(s32[643]{0:T(1024)S(1)} %concatenate.6.refs_0_, f32[640]{0:T(1024)S(1)} %pad_maximum_fusion.refs_1_, bf16[32,80,128]{2,1,0:T(8,128)(2,1)S(1)} %collective-permute-done.refs_2_, bf16[32,80,128]{2,1,0:T(8,128)(2,1)S(1)} %collective-permute-done.1.refs_3_, ...), custom_call_target="tpu_custom_call" | custom-call | flops 6000000000 | bytes 3000000 | tf_op jit(solution)/shard_map/gram/pallas_call | solution.py:201
  46.3 0.0 all-to-all-done
  46.3 4.4 %all-to-all-start.1 = ((bf16[80,8,80]{2,1,0:T(8,128)(2,1)}), bf16[80,8,80]{2,1,0:T(8,128)(2,1)S(1)}, u32[]{:S(2)}, u32[]{:S(2)}) async-start(bf16[80,8,80]{2,1,0:T(8,128)(2,1)} %get-tuple-element.5), calls=%async_computation.1 | async-start | bytes 327680 | tf_op jit(solution)/shard_map/all_to_all | solution.py:215
  50.7 3.7 %fusion = bf16[80,32,128]{0,1,2:T(8,128)(2,1)} fusion(bf16[128,80,128]{2,1,0:T(8,128)(2,1)S(1)} %get-tuple-element.4, bf16[128,32,128]{2,1,0:T(8,128)(2,1)} %bitcast.9, f32[128]{0:T(128)S(1)} %compare_convert_fusion), kind=kOutput, calls=%fused_computation.1 | convolution fusion | flops 84541440 | bytes 4325888 | tf_op jit(solution)/shard_map/ncl,nml->mcn/dot_general | solution.py:216
  54.4 3.0 %copy.9 = bf16[80,32,128]{2,1,0:T(8,128)(2,1)} copy(bf16[80,32,128]{0,1,2:T(8,128)(2,1)} %fusion) | data formatting | bytes 1310720
  57.4 0.0 all-to-all-done.1
  57.4 0.7 %convert_reduce_fusion = f32[10,8,80]{2,1,0:T(8,128)} fusion(bf16[8,10,8,80]{3,2,1,0:T(8,128)(2,1)S(1)} %bitcast.31), kind=kLoop, calls=%fused_computation.3 | loop fusion | flops 96000 | bytes 128000 | tf_op jit(solution)/shard_map/reduce_sum | solution.py:220
  (9 shorter events, 0.1 us)
Async XLA Ops:
  0.6 23.7 %copy-start.1 = (bf16[16,256,128]{2,1,0:T(8,128)(2,1)S(1)}, bf16[16,256,128]{2,1,0:T(8,128)(2,1)}, u32[]{:S(2)}) copy-start(bf16[16,256,128]{2,1,0:T(8,128)(2,1)} %refs_5_.1) | copy-start | bytes 3145732
  2.7 27.9 %copy-start.4 = (f32[128,4]{0,1:T(4,128)S(1)}, f32[128,4]{0,1:T(4,128)}, u32[]{:S(2)}) copy-start(f32[128,4]{0,1:T(4,128)} %param.9) | copy-start | bytes 6148
  2.7 27.9 %copy-start.5 = (s32[128,4]{0,1:T(4,128)S(1)}, s32[128,4]{0,1:T(4,128)}, u32[]{:S(2)}) copy-start(s32[128,4]{0,1:T(4,128)} %param.8) | copy-start | bytes 6148
  2.7 29.5 %collective-permute-start = (bf16[32,80,128]{2,1,0:T(8,128)(2,1)}, bf16[32,80,128]{2,1,0:T(8,128)(2,1)S(1)}, u32[]{:S(2)}, u32[]{:S(2)}) collective-permute-start(bf16[32,80,128]{2,1,0:T(8,128)(2,1)} %edge.1), channel_id=1, source_target_pairs={{0,8},{1,1017},{2,10},{3,1019},{4,12},{5,1021},{6,14},{7,1023},{8,... | collective-permute-start | bytes 1966088 | tf_op jit(solution)/shard_map/ppermute | solution.py:162
  25.5 20.8 %all-to-all-start = ((bf16[8,16,32,128]{3,2,1,0:T(8,128)(2,1)}), bf16[8,16,32,128]{3,2,1,0:T(8,128)(2,1)}, u32[]{:S(2)}, u32[]{:S(2)}) async-start(bf16[8,16,32,128]{3,2,1,0:T(8,128)(2,1)} %bitcast.27), calls=%async_computation | async-start | bytes 2097152 | tf_op jit(solution)/shard_map/all_to_all | solution.py:166
  32.2 9.4 %collective-permute-start.1 = (bf16[32,80,128]{2,1,0:T(8,128)(2,1)S(1)}, bf16[32,80,128]{2,1,0:T(8,128)(2,1)S(1)}, u32[]{:S(2)}, u32[]{:S(2)}) collective-permute-start(bf16[32,80,128]{2,1,0:T(8,128)(2,1)S(1)} %collective-permute-done.refs_2_), channel_id=1, source_target_pairs={{0,1},{1,0},{2,3},{3,2},{4,5},{5,4},{6,7},{7,6},{8,9},{9,8},{10,11... | collective-permute-start | bytes 1966088 | tf_op jit(solution)/shard_map/ppermute | solution.py:163
  36.0 2.5 %copy-start = (bf16[256,80,128]{2,1,0:T(8,128)(2,1)S(1)}, bf16[256,80,128]{2,1,0:T(8,128)(2,1)}, u32[]{:S(2)}) copy-start(bf16[256,80,128]{2,1,0:T(8,128)(2,1)} %refs_2_.1) | copy-start | bytes 15728644
  38.5 3.1 %copy-start.2 = (bf16[16,256,128]{2,1,0:T(8,128)(2,1)S(1)}, bf16[16,256,128]{2,1,0:T(8,128)(2,1)}, u32[]{:S(2)}) copy-start(bf16[16,256,128]{2,1,0:T(8,128)(2,1)} %refs_5_.1) | copy-start | bytes 3145732
  38.5 3.1 %copy-start.3 = (bf16[256,16]{0,1:T(8,128)(2,1)S(1)}, bf16[256,16]{0,1:T(8,128)(2,1)}, u32[]{:S(2)}) copy-start(bf16[256,16]{0,1:T(8,128)(2,1)} %param.11) | copy-start | bytes 24580
  46.3 11.1 %all-to-all-start.1 = ((bf16[80,8,80]{2,1,0:T(8,128)(2,1)}), bf16[80,8,80]{2,1,0:T(8,128)(2,1)S(1)}, u32[]{:S(2)}, u32[]{:S(2)}) async-start(bf16[80,8,80]{2,1,0:T(8,128)(2,1)} %get-tuple-element.5), calls=%async_computation.1 | async-start | bytes 327680 | tf_op jit(solution)/shard_map/all_to_all | solution.py:215

commit v3 on v2

--- a/solution.py
+++ b/solution.py
@@ -12,6 +12,11 @@
 PTS = 8
 FP = 4
 MIB = 1024 * 1024
+REACH = FP * OBS_DEV
+TAIL = REACH + OBS_DEV
+HOME_COLS = TAIL + 2
+LOCALITY = FP * OBS_DEV
+HOME_GAINS = LOCALITY + OBS_DEV
 
 VMEM = pltpu.MemorySpace.VMEM
 SMEM = pltpu.MemorySpace.SMEM
@@ -33,17 +38,6 @@
     return jnp.where(relative <= 1.0, near_part, jnp.where(relative <= 2.0, far_part, 0.0))
 
 
-def home_mix(ints, gains, anomaly, n, tile_cols):
-    total = None
-    for f in range(FP):
-        col = ints[f * OBS_DEV + n] - HALO
-        inside = jnp.logical_and(col >= 0, col < tile_cols)
-        gain = jnp.where(inside, gains[f * OBS_DEV + n], 0.0)
-        term = gain * anomaly[jnp.clip(col, 0, tile_cols - 1)].astype(jnp.float32)
-        total = term if total is None else total + term
-    return total
-
-
 def side_mix(ints, gains, halo, n, first):
     total = None
     for f in range(FP):
@@ -55,38 +49,45 @@
     return total
 
 
-def edge_kernel(anomaly, edge, sem):
-    core = lax.rem(lax.axis_index("chan"), 2)
-    first = jnp.where(core == 0, anomaly.shape[0] - HALO, 0)
-    copy = pltpu.make_async_copy(anomaly.at[pl.ds(first, HALO)], edge, sem)
-    copy.start()
-    copy.wait()
-
-
-def home_kernel(tile_cols, ints, gains, anomaly, home):
-    def each(n, carry):
-        home[n] = home_mix(ints, gains, anomaly, n, tile_cols).astype(home.dtype)
-        return carry
-
-    lax.fori_loop(0, OBS_DEV, each, 0, unroll=4)
-
-
-def gram_kernel(tile_cols, ints, gains, ours, theirs, home, jac, weight, gram, mixed, perts, products, turned):
+def home_kernel(ints, gains, anomaly, home, tile, sems):
+    members = anomaly.shape[1]
+    cuts = (0, 48, members)
+    parts = [pl.ds(low, high - low) for low, high in zip(cuts, cuts[1:])]
+    copies = [
+        pltpu.make_async_copy(anomaly.at[:, part], tile.at[:, part], sems.at[k])
+        for k, part in enumerate(parts)
+    ]
+    for copy in copies:
+        copy.start()
+    for copy, part in zip(copies, parts):
+        copy.wait()
+
+        def each(n, carry, part=part):
+            total = None
+            for f in range(FP):
+                gain = gains[HOME_GAINS + f * OBS_DEV + n]
+                term = gain * tile[ints[HOME_COLS + f * OBS_DEV + n], part].astype(jnp.float32)
+                total = term if total is None else total + term
+            home[n, part] = total.astype(home.dtype)
+            return carry
+
+        lax.fori_loop(0, OBS_DEV, each, 0, unroll=4)
+
+
+def gram_kernel(tile_cols, count, ints, gains, ours, theirs, home, jac, weight, gram, mixed, perts, products, turned):
     share, members = perts.shape[:2]
-    tail = (FP + 1) * OBS_DEV
-    first_obs = ints[tail]
-    live_count = ints[tail + 1]
-    first_ours = ints[tail + 2]
+    first_obs = ints[TAIL]
+    live_count = count[0]
+    first_ours = ints[TAIL + 1]
     first_theirs = HALO + tile_cols - first_ours
-    mixed[...] = home[...]
 
     def add(n, halo, first):
         mixed[n] = (mixed[n].astype(jnp.float32) + side_mix(ints, gains, halo, n, first)).astype(
             mixed.dtype
         )
 
-    def each(n, carry):
-        reach = ints[FP * OBS_DEV + n]
+    def complete(n):
+        reach = ints[REACH + n]
 
         @pl.when(reach > 0)
         def _():
@@ -98,9 +99,14 @@
             def _():
                 add(n, theirs, first_theirs)
 
+    def each(q, carry):
+        batch = pl.ds(q * 4, 4)
+        mixed[batch] = home[batch]
+        for k in range(4):
+            complete(q * 4 + k)
         return carry
 
-    lax.fori_loop(0, OBS_DEV, each, 0, unroll=4)
+    lax.fori_loop(0, OBS_DEV // 4, each, 0)
     for i in range(share):
         live = jnp.where(first_obs + i < live_count, 1.0, 0.0)
         radiance = lax.dot_general(
@@ -116,10 +122,71 @@
     for p in range(PTS):
         total = None
         for i in range(share):
-            term = gains[FP * OBS_DEV + p * share + i] * products[i]
+            term = gains[LOCALITY + p * share + i] * products[i]
             total = term if total is None else total + term
         turned[pl.ds(p, members, stride=PTS), 0:members] = total
     gram[...] = turned[:, 0:members].reshape(members, PTS, members).astype(gram.dtype)
+
+
+def radiance_kernel(count, jac, mixed_ref, out, mixed, turned, sems):
+    members, block, levels = mixed.shape[1], jac.shape[1], jac.shape[2]
+    steps = sems.shape[0]
+    packs = levels // block
+    groups = OBS_DEV // packs
+    pitch = groups + 8
+    owner = lax.broadcasted_iota(jnp.int32, (members, levels), 1) // block
+
+    batch = groups // steps
+    copies = [
+        [
+            pltpu.make_async_copy(
+                mixed_ref.at[pl.ds(j * groups + step * batch, batch)],
+                mixed.at[pl.ds(j * groups + step * batch, batch)],
+                sems.at[step, j],
+            )
+            for j in range(packs)
+        ]
+        for step in range(steps)
+    ]
+    for step in copies:
+        for copy in step:
+            copy.start()
+
+    def group(g, carry):
+        names = [g + j * groups for j in range(packs)]
+        stacked = jnp.concatenate([jac[n] for n in names], axis=0)
+        kept = None
+        for j, n in enumerate(names):
+            part = lax.dot_general(mixed[n], stacked, NT, preferred_element_type=jnp.float32)
+            kept = part if kept is None else jnp.where(owner == j, part, kept)
+        turned[pl.ds(g, members, stride=pitch), :] = kept
+        return carry
+
+    for step in range(steps):
+        for copy in copies[step]:
+            copy.wait()
+        lax.fori_loop(step * batch, (step + 1) * batch, group, 0, unroll=4)
+    slot = lax.broadcasted_iota(jnp.int32, (block, OBS_DEV), 1)
+    spot = slot // groups
+    live = slot < count[0]
+
+    def members_of(q, carry):
+        rows = [
+            turned[pl.ds(pl.multiple_of((q * packs + k) * pitch, 8), groups), :]
+            for k in range(packs)
+        ]
+        flipped = jnp.concatenate(rows, axis=0).T
+        for k in range(packs):
+            kept = None
+            for j in range(packs):
+                piece = flipped[j * block : (j + 1) * block, :]
+                shift = (j - k) * groups % OBS_DEV
+                piece = piece if shift == 0 else pltpu.roll(piece, shift, 1)
+                kept = piece if kept is None else jnp.where(spot == j, piece, kept)
+            out[q * packs + k] = jnp.where(live, kept, 0.0).astype(out.dtype)
+        return carry
+
+    lax.fori_loop(0, members // packs, members_of, 0, unroll=2)
 
 
 def params(mib):
@@ -144,16 +211,9 @@
     block = CH // chans
 
     core = lax.rem(chan_index, 2)
-    edge = pl.pallas_call(
-        edge_kernel,
-        out_shape=jax.ShapeDtypeStruct((HALO, members, levels), jnp.bfloat16),
-        in_specs=specs(pl.ANY),
-        out_specs=pl.BlockSpec(memory_space=VMEM),
-        scratch_shapes=[pltpu.SemaphoreType.DMA],
-        compiler_params=params(59),
-        cost_estimate=cost(1_000_000, 1_300_000),
-        name="edge",
-    )(anomaly)
+    edge = lax.dynamic_slice_in_dim(
+        anomaly, jnp.where(core == 0, tile_cols - HALO, 0), HALO, 0
+    )
     to_side = [
         (t * chans + j, (t + (1 if j % 2 == 0 else -1)) % col_groups * chans + j)
         for t in range(col_groups)
@@ -183,17 +243,23 @@
     ours_reach = jnp.where(core == 0, low_reach, high_reach)
     theirs_reach = jnp.where(core == 0, high_reach, low_reach)
     reach = ours_reach.astype(jnp.int32) + 2 * theirs_reach.astype(jnp.int32)
-    tail = jnp.stack([first_obs, obs_count[0], first_ours]).astype(jnp.int32)
-    ints = jnp.concatenate([offsets.reshape(-1), reach, tail])
-    gains = jnp.concatenate([column_gains.reshape(-1), locality.reshape(-1)])
+    tail = jnp.stack([first_obs, first_ours]).astype(jnp.int32)
+    inside = jnp.logical_and(offsets >= HALO, offsets < HALO + tile_cols)
+    home_cols = jnp.clip(offsets - HALO, 0, tile_cols - 1)
+    home_gains = jnp.where(inside, column_gains, 0.0)
+    ints = jnp.concatenate([offsets.reshape(-1), reach, tail, home_cols.reshape(-1)])
+    gains = jnp.concatenate(
+        [column_gains.reshape(-1), locality.reshape(-1), home_gains.reshape(-1)]
+    )
 
     tile = jax.ShapeDtypeStruct((OBS_DEV, members, levels), jnp.bfloat16)
     home = pl.pallas_call(
-        lambda *refs: home_kernel(tile_cols, *refs),
+        home_kernel,
         out_shape=tile,
-        in_specs=specs(SMEM, SMEM, VMEM),
+        in_specs=specs(SMEM, SMEM, pl.ANY),
         out_specs=pl.BlockSpec(memory_space=VMEM),
-        compiler_params=params(12),
+        scratch_shapes=[pltpu.VMEM(anomaly.shape, anomaly.dtype), pltpu.SemaphoreType.DMA((2,))],
+        compiler_params=params(50),
         cost_estimate=cost(4_000_000_000, 8_000_000),
         name="home_mix",
     )(ints, gains, anomaly)
@@ -201,7 +267,7 @@
     gram, mixed = pl.pallas_call(
         lambda *refs: gram_kernel(tile_cols, *refs),
         out_shape=(jax.ShapeDtypeStruct((members, PTS, members), jnp.bfloat16), tile),
-        in_specs=specs(SMEM, SMEM, VMEM, VMEM, VMEM, VMEM, VMEM),
+        in_specs=specs(SMEM, SMEM, SMEM, VMEM, VMEM, VMEM, VMEM, VMEM),
         out_specs=tuple(specs(VMEM, VMEM)),
         scratch_shapes=[
             pltpu.VMEM((obs_share, members, CH), jnp.bfloat16),
@@ -211,11 +277,22 @@
         compiler_params=params(16),
         cost_estimate=cost(6_000_000_000, 3_000_000),
         name="gram",
-    )(ints, gains, ours, theirs, home, jacobian, obs_weight.T)
+    )(obs_count, ints, gains, ours, theirs, home, jacobian, obs_weight.T)
     arrived = lax.all_to_all(gram, "chan", split_axis=0, concat_axis=0, tiled=True)
-    radiance = jnp.einsum("ncl,nml->mcn", jac_block, mixed, preferred_element_type=jnp.float32)
-    live_mask = (jnp.arange(OBS_DEV, dtype=jnp.int32) < obs_count[0]).astype(jnp.float32)
-    perturbed = (radiance * live_mask[None, None, :]).astype(jnp.bfloat16)
+    perturbed = pl.pallas_call(
+        radiance_kernel,
+        out_shape=jax.ShapeDtypeStruct((members, block, OBS_DEV), jnp.bfloat16),
+        in_specs=specs(SMEM, VMEM, pl.ANY),
+        out_specs=pl.BlockSpec(memory_space=VMEM),
+        scratch_shapes=[
+            pltpu.VMEM(tile.shape, tile.dtype),
+            pltpu.VMEM((members * (OBS_DEV * block // levels + 8), levels), jnp.float32),
+            pltpu.SemaphoreType.DMA((4, levels // block)),
+        ],
+        compiler_params=params(52),
+        cost_estimate=cost(4_000_000_000, 5_000_000),
+        name="radiance",
+    )(obs_count, jac_block, mixed)
 
     gram_rows = arrived.reshape(chans, members // chans, PTS, members).astype(jnp.float32).sum(0)
     return perturbed, gram_rows.transpose(1, 0, 2)

time: 58.5 us -> 60.1 us (1.027)
  Pallas kernels: 9.74 us -> 18.1 us
  matrix products: 3.74 us -> 0 us
  local copies, waits for them, and re-layouts: 7.01 us -> 5.39 us
  waiting for transfers between devices: 1.01 us -> 0.01 us
    pallas_call x2, Pallas kernels: 5.14 us -> 13.6 us  [the longest x1 8.27 us: shards(): pl.pallas_call(radiance_kernel, out_shape=jax.ShapeDtypeStruct((members,...]
    unnamed x13 -> x10, local copies, waits for them, and re-layouts: 5.48 us -> 1.54 us
    dot_general x1 -> x0, matrix products: 3.74 us -> none  [shards(): jnp.einsum('ncl,nml->mcn', jac_block, mixed, preferred_element_type=jnp.f...]
    reshape x1, local copies, waits for them, and re-layouts: 1.12 us -> 2.31 us  [shards(): jacobian.reshape(obs_share, chans, block, levels).transpose(1, 0, 2, 3)]
    dynamic_slice x0 -> x1, local copies, waits for them, and re-layouts: none -> 1.13 us  [shards(): lax.dynamic_slice_in_dim(anomaly, jnp.where(core == 0, tile_cols - HALO,...]
    ppermute x1, waiting for transfers between devices: 1.01 us -> 0.01 us  [shards(): ours = lax.ppermute(edge, ('cols', 'chan'), to_side)]
  transfers between devices with their start and end apart: 4 -> 4, of which waited for: 1 -> 0; matrix products, arithmetic and copies ran while one was open for 15% -> 5% of each run, Pallas kernels for 13% -> 30%
where the time goes in v3:
time: 60.1 us; the launch traced here: 59.7 us
  starting transfers between devices  33.9 us (56%)
  Pallas kernels  18.1 us (30%)
  local copies, waits for them, and re-layouts  5.39 us (9%)
  between operations  1.45 us (2%)
  other arithmetic  0.86 us (1%)
    ppermute x1, starting transfers between devices, shards(): ours = lax.ppermute(edge, ('cols', 'chan'), to_side)  21.7 us
    pallas_call x1, Pallas kernels, shards(): pl.pallas_call(radiance_kernel, out_shape=jax.ShapeDtypeStruct((members,...  8.27 us
    pallas_call x1, Pallas kernels, shards(): pl.pallas_call(home_kernel, out_shape=tile, in_specs=specs(SMEM, SMEM, pl...  5.28 us
    pallas_call x1, Pallas kernels, shards(): pl.pallas_call(lambda *refs: gram_kernel(tile_cols, *refs), out_shape=(ja...  4.52 us
    all_to_all x1, starting transfers between devices, shards(): lax.all_to_all(pieces, 'chan', split_axis=0, concat_axis=0, tiled=True)  4.41 us
    all_to_all x1, starting transfers between devices, shards(): lax.all_to_all(gram, 'chan', split_axis=0, concat_axis=0, tiled=True)  4.41 us
    ppermute x1, starting transfers between devices, shards(): theirs = lax.ppermute(ours, 'chan', [(j, j ^ 1) for j in range(chans)])  3.39 us
    reshape x1, local copies, waits for them, and re-layouts, shards(): jacobian.reshape(obs_share, chans, block, levels).transpose(1, 0, 2, 3)  2.31 us
  transfers between devices with their start and end apart: 4, of which 0 were waited for; matrix products, arithmetic and copies ran while one was open for 5% of the time, Pallas kernels for 30%

profile of v3, /device:TPU:1, one launch (start us, length us, event | category | flops | bytes accessed | tf_op | source)
XLA Modules:
  0.0 59.7 jit_solution(16728081595086043338)
XLA Ops:
  0.6 0.0 copy-start.3
  0.6 0.0 copy-start.4
  0.7 1.1 %constant_dynamic-slice_fusion = bf16[32,80,128]{2,1,0:T(8,128)(2,1)S(1)} fusion(bf16[256,80,128]{2,1,0:T(8,128)(2,1)} %anomaly.1, s32[]{:T(128)S(6)} %select_n.53), kind=kLoop, calls=%fused_computation.26 | loop fusion | bytes 1310724 | tf_op jit(solution)/shard_map/dynamic_slice | solution.py:214
  1.8 21.7 %collective-permute-start = (bf16[32,80,128]{2,1,0:T(8,128)(2,1)S(1)}, bf16[32,80,128]{2,1,0:T(8,128)(2,1)S(1)}, u32[]{:S(2)}, u32[]{:S(2)}) collective-permute-start(bf16[32,80,128]{2,1,0:T(8,128)(2,1)S(1)} %constant_dynamic-slice_fusion), channel_id=1, source_target_pairs={{0,8},{1,1017},{2,10},{3,1019},{4,12},{5,1021},{6,14},{7,1023},{8,... | collective-permute-start | bytes 1966088 | tf_op jit(solution)/shard_map/ppermute | solution.py:222
  23.5 2.3 %copy.10 = bf16[16,8,32,128]{3,2,0,1:T(8,128)(2,1)} copy(bf16[16,8,32,128]{3,2,1,0:T(8,128)(2,1)} %bitcast.30) | data formatting | bytes 2097152 | tf_op jit(solution)/shard_map/reshape | solution.py:225
  25.8 4.4 %all-to-all-start = ((bf16[8,16,32,128]{3,2,1,0:T(8,128)(2,1)}), bf16[8,16,32,128]{3,2,1,0:T(8,128)(2,1)S(1)}, u32[]{:S(2)}, u32[]{:S(2)}) async-start(bf16[8,16,32,128]{3,2,1,0:T(8,128)(2,1)} %bitcast.29), calls=%async_computation | async-start | bytes 2097152 | tf_op jit(solution)/shard_map/all_to_all | solution.py:226
  30.2 0.0 copy-done.3
  30.2 0.0 copy-done.4
  30.3 0.1 dynamic_slice.6
  30.4 0.1 multiply_add_fusion.1
  30.4 0.1 add.71
  30.5 0.1 div.30
  30.6 0.1 sub.50
  31.4 0.1 concatenate.6.ints.refs_1_
  31.5 0.0 collective-permute-done.refs_3_
  31.5 3.4 %collective-permute-start.1 = (bf16[32,80,128]{2,1,0:T(8,128)(2,1)S(1)}, bf16[32,80,128]{2,1,0:T(8,128)(2,1)S(1)}, u32[]{:S(2)}, u32[]{:S(2)}) collective-permute-start(bf16[32,80,128]{2,1,0:T(8,128)(2,1)S(1)} %collective-permute-done.refs_3_), channel_id=1, source_target_pairs={{0,1},{1,0},{2,3},{3,2},{4,5},{5,4},{6,7},{7,6},{8,9},{9,8},{10,11... | collective-permute-start | bytes 1966088 | tf_op jit(solution)/shard_map/ppermute | solution.py:223
  34.9 0.0 copy-start
  34.9 0.0 copy-start.1
  34.9 5.3 %home_mix.1.refs_5_ = bf16[128,80,128]{2,1,0:T(8,128)(2,1)S(1)} custom-call(s32[1154]{0:T(1024)S(1)} %concatenate.6.ints.refs_1_, f32[1152]{0:T(1024)S(1)} %pad_maximum_fusion.gains.refs_2_, bf16[256,80,128]{2,1,0:T(8,128)(2,1)} %anomaly.1), custom_call_target="tpu_custom_call" | custom-call | flops 4000000000 | bytes 8000000 | tf_op jit(solution)/shard_map/home_mix/pallas_call | solution.py:256
  40.2 0.0 collective-permute-done.1.refs_4_
  40.2 0.0 copy-done
  40.3 0.0 copy-done.1
  40.3 4.5 %gram.1 = (bf16[80,8,80]{2,1,0:T(8,128)(2,1)}, bf16[128,80,128]{2,1,0:T(8,128)(2,1)S(1)}) custom-call(s32[1]{0:T(128)S(6)} %copy.11.refs_0_.count, s32[1154]{0:T(1024)S(1)} %concatenate.6.ints.refs_1_, f32[1152]{0:T(1024)S(1)} %pad_maximum_fusion.gains.refs_2_, bf16[32,80,128]{2,1,0:T(8,128)(2,1)S(1)} %collective-permute-done.refs_3_, ...), custom_call_target="tpu_custom_call" | custom-call | flops 6000000000 | bytes 3000000 | tf_op jit(solution)/shard_map/gram/pallas_call | solution.py:267
  44.8 0.0 copy-start.2
  44.8 1.5 %copy-done.2 = bf16[128,80,128]{2,1,0:T(8,128)(2,1)} copy-done((bf16[128,80,128]{2,1,0:T(8,128)(2,1)}, bf16[128,80,128]{2,1,0:T(8,128)(2,1)S(1)}, u32[]{:S(2)}) %copy-start.2) | copy-done | bytes 2621464
  46.3 0.0 all-to-all-done
  46.3 4.4 %all-to-all-start.1 = ((bf16[80,8,80]{2,1,0:T(8,128)(2,1)}), bf16[80,8,80]{2,1,0:T(8,128)(2,1)S(1)}, u32[]{:S(2)}, u32[]{:S(2)}) async-start(bf16[80,8,80]{2,1,0:T(8,128)(2,1)} %get-tuple-element.5), calls=%async_computation.1 | async-start | bytes 327680 | tf_op jit(solution)/shard_map/all_to_all | solution.py:281
  50.7 8.3 %radiance.1 = bf16[80,32,128]{2,1,0:T(8,128)(2,1)} custom-call(s32[1]{0:T(128)S(6)} %copy.11.refs_0_.count, bf16[128,32,128]{2,1,0:T(8,128)(2,1)S(1)} %bitcast.31, bf16[128,80,128]{2,1,0:T(8,128)(2,1)} %copy-done.2), custom_call_target="tpu_custom_call" | custom-call | flops 4000000000 | bytes 5000000 | tf_op jit(solution)/shard_map/radiance/pallas_call | solution.py:282
  59.0 0.0 all-to-all-done.1
  59.0 0.7 %convert_reduce_fusion = f32[10,8,80]{2,1,0:T(8,128)} fusion(bf16[8,10,8,80]{3,2,1,0:T(8,128)(2,1)S(1)} %bitcast.33), kind=kLoop, calls=%fused_computation.1 | loop fusion | flops 96000 | bytes 128000 | tf_op jit(solution)/shard_map/reduce_sum | solution.py:297
  (9 shorter events, 0.1 us)
Async XLA Ops:
  0.6 29.6 %copy-start.3 = (f32[128,4]{0,1:T(4,128)S(1)}, f32[128,4]{0,1:T(4,128)}, u32[]{:S(2)}) copy-start(f32[128,4]{0,1:T(4,128)} %param.9) | copy-start | bytes 6148
  0.6 29.6 %copy-start.4 = (s32[128,4]{0,1:T(4,128)S(1)}, s32[128,4]{0,1:T(4,128)}, u32[]{:S(2)}) copy-start(s32[128,4]{0,1:T(4,128)} %param.8) | copy-start | bytes 6148
  1.8 29.7 %collective-permute-start = (bf16[32,80,128]{2,1,0:T(8,128)(2,1)S(1)}, bf16[32,80,128]{2,1,0:T(8,128)(2,1)S(1)}, u32[]{:S(2)}, u32[]{:S(2)}) collective-permute-start(bf16[32,80,128]{2,1,0:T(8,128)(2,1)S(1)} %constant_dynamic-slice_fusion), channel_id=1, source_target_pairs={{0,8},{1,1017},{2,10},{3,1019},{4,12},{5,1021},{6,14},{7,1023},{8,... | collective-permute-start | bytes 1966088 | tf_op jit(solution)/shard_map/ppermute | solution.py:222
  25.8 20.5 %all-to-all-start = ((bf16[8,16,32,128]{3,2,1,0:T(8,128)(2,1)}), bf16[8,16,32,128]{3,2,1,0:T(8,128)(2,1)S(1)}, u32[]{:S(2)}, u32[]{:S(2)}) async-start(bf16[8,16,32,128]{3,2,1,0:T(8,128)(2,1)} %bitcast.29), calls=%async_computation | async-start | bytes 2097152 | tf_op jit(solution)/shard_map/all_to_all | solution.py:226
  31.5 8.8 %collective-permute-start.1 = (bf16[32,80,128]{2,1,0:T(8,128)(2,1)S(1)}, bf16[32,80,128]{2,1,0:T(8,128)(2,1)S(1)}, u32[]{:S(2)}, u32[]{:S(2)}) collective-permute-start(bf16[32,80,128]{2,1,0:T(8,128)(2,1)S(1)} %collective-permute-done.refs_3_), channel_id=1, source_target_pairs={{0,1},{1,0},{2,3},{3,2},{4,5},{5,4},{6,7},{7,6},{8,9},{9,8},{10,11... | collective-permute-start | bytes 1966088 | tf_op jit(solution)/shard_map/ppermute | solution.py:223
  34.9 5.3 %copy-start = (bf16[16,256,128]{2,1,0:T(8,128)(2,1)S(1)}, bf16[16,256,128]{2,1,0:T(8,128)(2,1)}, u32[]{:S(2)}) copy-start(bf16[16,256,128]{2,1,0:T(8,128)(2,1)} %refs_6_.1) | copy-start | bytes 3145732
  34.9 5.3 %copy-start.1 = (bf16[256,16]{0,1:T(8,128)(2,1)S(1)}, bf16[256,16]{0,1:T(8,128)(2,1)}, u32[]{:S(2)}) copy-start(bf16[256,16]{0,1:T(8,128)(2,1)} %param.11) | copy-start | bytes 24580
  44.8 1.5 %copy-start.2 = (bf16[128,80,128]{2,1,0:T(8,128)(2,1)}, bf16[128,80,128]{2,1,0:T(8,128)(2,1)S(1)}, u32[]{:S(2)}) copy-start(bf16[128,80,128]{2,1,0:T(8,128)(2,1)S(1)} %get-tuple-element.4.mixed_ref) | copy-start | bytes 7864324
  46.3 12.7 %all-to-all-start.1 = ((bf16[80,8,80]{2,1,0:T(8,128)(2,1)}), bf16[80,8,80]{2,1,0:T(8,128)(2,1)S(1)}, u32[]{:S(2)}, u32[]{:S(2)}) async-start(bf16[80,8,80]{2,1,0:T(8,128)(2,1)} %get-tuple-element.5), calls=%async_computation.1 | async-start | bytes 327680 | tf_op jit(solution)/shard_map/all_to_all | solution.py:281

commit v4 on v3

--- a/solution.py
+++ b/solution.py
@@ -49,6 +49,32 @@
     return total
 
 
+def prepare_kernel(anomaly, jac, edge, pieces, cut, held, cut_sems, in_sems, out_sems):
+    core = lax.rem(lax.axis_index("chan"), 2)
+    first = jnp.where(core == 0, anomaly.shape[0] - HALO, 0)
+    chans, _, block, _ = held.shape
+    cut_in = pltpu.make_async_copy(anomaly.at[pl.ds(first, HALO)], cut, cut_sems.at[0])
+    cut_out = pltpu.make_async_copy(cut, edge, cut_sems.at[1])
+    cut_in.start()
+    arrive = [
+        pltpu.make_async_copy(jac.at[:, pl.ds(j * block, block)], held.at[j], in_sems.at[j])
+        for j in range(chans)
+    ]
+    leave = [
+        pltpu.make_async_copy(held.at[j], pieces.at[j], out_sems.at[j]) for j in range(chans)
+    ]
+    for copy in arrive:
+        copy.start()
+    cut_in.wait()
+    cut_out.start()
+    for before, after in zip(arrive, leave):
+        before.wait()
+        after.start()
+    cut_out.wait()
+    for copy in leave:
+        copy.wait()
+
+
 def home_kernel(ints, gains, anomaly, home, tile, sems):
     members = anomaly.shape[1]
     cuts = (0, 48, members)
@@ -74,7 +100,7 @@
         lax.fori_loop(0, OBS_DEV, each, 0, unroll=4)
 
 
-def gram_kernel(tile_cols, count, ints, gains, ours, theirs, home, jac, weight, gram, mixed, perts, products, turned):
+def gram_kernel(tile_cols, count, ints, gains, ours, theirs, home, jac, weight, gram, mixed_out, mixed, perts, products, turned, sem):
     share, members = perts.shape[:2]
     first_obs = ints[TAIL]
     live_count = count[0]
@@ -107,6 +133,8 @@
         return carry
 
     lax.fori_loop(0, OBS_DEV // 4, each, 0)
+    leave = pltpu.make_async_copy(mixed, mixed_out, sem)
+    leave.start()
     for i in range(share):
         live = jnp.where(first_obs + i < live_count, 1.0, 0.0)
         radiance = lax.dot_general(
@@ -126,6 +154,7 @@
             total = term if total is None else total + term
         turned[pl.ds(p, members, stride=PTS), 0:members] = total
     gram[...] = turned[:, 0:members].reshape(members, PTS, members).astype(gram.dtype)
+    leave.wait()
 
 
 def radiance_kernel(count, jac, mixed_ref, out, mixed, turned, sems):
@@ -155,24 +184,25 @@
     def group(g, carry):
         names = [g + j * groups for j in range(packs)]
         stacked = jnp.concatenate([jac[n] for n in names], axis=0)
-        kept = None
-        for j, n in enumerate(names):
-            part = lax.dot_general(mixed[n], stacked, NT, preferred_element_type=jnp.float32)
-            kept = part if kept is None else jnp.where(owner == j, part, kept)
+        averages = jnp.concatenate([mixed[n] for n in names], axis=0)
+        full = lax.dot_general(averages, stacked, NT, preferred_element_type=jnp.float32)
+        kept = full[:members]
+        for j in range(1, packs):
+            kept = jnp.where(owner == j, full[j * members : (j + 1) * members], kept)
         turned[pl.ds(g, members, stride=pitch), :] = kept
         return carry
 
     for step in range(steps):
         for copy in copies[step]:
             copy.wait()
-        lax.fori_loop(step * batch, (step + 1) * batch, group, 0, unroll=4)
+        lax.fori_loop(step * batch, (step + 1) * batch, group, 0, unroll=batch)
     slot = lax.broadcasted_iota(jnp.int32, (block, OBS_DEV), 1)
     spot = slot // groups
     live = slot < count[0]
 
     def members_of(q, carry):
         rows = [
-            turned[pl.ds(pl.multiple_of((q * packs + k) * pitch, 8), groups), :]
+            turned[pl.ds(pl.multiple_of((q * packs + k) * pitch, 8), groups), :].astype(out.dtype)
             for k in range(packs)
         ]
         flipped = jnp.concatenate(rows, axis=0).T
@@ -183,10 +213,10 @@
                 shift = (j - k) * groups % OBS_DEV
                 piece = piece if shift == 0 else pltpu.roll(piece, shift, 1)
                 kept = piece if kept is None else jnp.where(spot == j, piece, kept)
-            out[q * packs + k] = jnp.where(live, kept, 0.0).astype(out.dtype)
+            out[q * packs + k] = jnp.where(live, kept, jnp.zeros_like(kept))
         return carry
 
-    lax.fori_loop(0, members // packs, members_of, 0, unroll=2)
+    lax.fori_loop(0, members // packs, members_of, 0, unroll=10)
 
 
 def params(mib):
@@ -211,9 +241,25 @@
     block = CH // chans
 
     core = lax.rem(chan_index, 2)
-    edge = lax.dynamic_slice_in_dim(
-        anomaly, jnp.where(core == 0, tile_cols - HALO, 0), HALO, 0
-    )
+    edge, pieces = pl.pallas_call(
+        prepare_kernel,
+        out_shape=(
+            jax.ShapeDtypeStruct((HALO, members, levels), jnp.bfloat16),
+            jax.ShapeDtypeStruct((chans, obs_share, block, levels), jnp.bfloat16),
+        ),
+        in_specs=specs(pl.ANY, pl.ANY),
+        out_specs=tuple(specs(pl.ANY, pl.ANY)),
+        scratch_shapes=[
+            pltpu.VMEM((HALO, members, levels), jnp.bfloat16),
+            pltpu.VMEM((chans, obs_share, block, levels), jnp.bfloat16),
+            pltpu.SemaphoreType.DMA((2,)),
+            pltpu.SemaphoreType.DMA((chans,)),
+            pltpu.SemaphoreType.DMA((chans,)),
+        ],
+        compiler_params=pltpu.CompilerParams(vmem_limit_bytes=int(60.4 * MIB)),
+        cost_estimate=cost(1_000_000, 3_000_000),
+        name="prepare",
+    )(anomaly, jacobian)
     to_side = [
         (t * chans + j, (t + (1 if j % 2 == 0 else -1)) % col_groups * chans + j)
         for t in range(col_groups)
@@ -222,7 +268,6 @@
     ours = lax.ppermute(edge, ("cols", "chan"), to_side)
     theirs = lax.ppermute(ours, "chan", [(j, j ^ 1) for j in range(chans)])
 
-    pieces = jacobian.reshape(obs_share, chans, block, levels).transpose(1, 0, 2, 3)
     jac_block = lax.all_to_all(pieces, "chan", split_axis=0, concat_axis=0, tiled=True)
     jac_block = jac_block.reshape(OBS_DEV, block, levels)
 
@@ -268,13 +313,15 @@
         lambda *refs: gram_kernel(tile_cols, *refs),
         out_shape=(jax.ShapeDtypeStruct((members, PTS, members), jnp.bfloat16), tile),
         in_specs=specs(SMEM, SMEM, SMEM, VMEM, VMEM, VMEM, VMEM, VMEM),
-        out_specs=tuple(specs(VMEM, VMEM)),
+        out_specs=tuple(specs(VMEM, pl.ANY)),
         scratch_shapes=[
+            pltpu.VMEM(tile.shape, tile.dtype),
             pltpu.VMEM((obs_share, members, CH), jnp.bfloat16),
             pltpu.VMEM((obs_share, members, members), jnp.float32),
             pltpu.VMEM((members * PTS, 128), jnp.float32),
+            pltpu.SemaphoreType.DMA,
         ],
-        compiler_params=params(16),
+        compiler_params=params(46),
         cost_estimate=cost(6_000_000_000, 3_000_000),
         name="gram",
     )(obs_count, ints, gains, ours, theirs, home, jacobian, obs_weight.T)
@@ -287,7 +334,7 @@
         scratch_shapes=[
             pltpu.VMEM(tile.shape, tile.dtype),
             pltpu.VMEM((members * (OBS_DEV * block // levels + 8), levels), jnp.float32),
-            pltpu.SemaphoreType.DMA((4, levels // block)),
+            pltpu.SemaphoreType.DMA((2, levels // block)),
         ],
         compiler_params=params(52),
         cost_estimate=cost(4_000_000_000, 5_000_000),

time: 60.1 us -> 64.2 us (1.068)
  waiting for transfers between devices: 0.01 us -> 8.06 us
  local copies, waits for them, and re-layouts: 5.39 us -> 1.93 us
  Pallas kernels: 18.1 us -> 16.8 us
  starting transfers between devices: 33.9 us -> 34.7 us
    all_to_all x1, starting transfers between devices: 4.41 us -> 17.6 us  [shards(): lax.all_to_all(pieces, 'chan', split_axis=0, concat_axis=0, tiled=True)]
    ppermute x1, starting transfers between devices: 21.7 us -> 9.05 us  [shards(): ours = lax.ppermute(edge, ('cols', 'chan'), to_side)]
    ppermute x1, waiting for transfers between devices: 0.01 us -> 6.54 us  [shards(): ours = lax.ppermute(edge, ('cols', 'chan'), to_side)]
    pallas_call x1, Pallas kernels: 8.27 us -> 4.03 us  [shards(): pl.pallas_call(radiance_kernel, out_shape=jax.ShapeDtypeStruct((members,...]
    pallas_call x0 -> x1, Pallas kernels: none -> 2.84 us  [shards(): pl.pallas_call(prepare_kernel, out_shape=(jax.ShapeDtypeStruct((HALO, mem...]
    reshape x1 -> x0, local copies, waits for them, and re-layouts: 2.31 us -> none  [shards(): jacobian.reshape(obs_share, chans, block, levels).transpose(1, 0, 2, 3)]
    all_to_all x1, waiting for transfers between devices: 0.01 us -> 1.51 us  [shards(): lax.all_to_all(gram, 'chan', split_axis=0, concat_axis=0, tiled=True)]
    dynamic_slice x1 -> x0, local copies, waits for them, and re-layouts: 1.13 us -> none  [shards(): lax.dynamic_slice_in_dim(anomaly, jnp.where(core == 0, tile_cols - HALO,...]
  transfers between devices with their start and end apart: 4 -> 4, of which waited for: 0 -> 2; matrix products, arithmetic and copies ran while one was open for 5% -> 1% of each run, Pallas kernels for 30% -> 22%
where the time goes in v4:
time: 64.2 us; the launch traced here: 63.8 us
  starting transfers between devices  34.7 us (54%)
  Pallas kernels  16.8 us (26%)
  waiting for transfers between devices  8.06 us (13%)
  local copies, waits for them, and re-layouts  1.93 us (3%)
  between operations  1.46 us (2%)
  other arithmetic  0.86 us (1%)
    all_to_all x1, starting transfers between devices, shards(): lax.all_to_all(pieces, 'chan', split_axis=0, concat_axis=0, tiled=True)  17.6 us
    ppermute x1, starting transfers between devices, shards(): ours = lax.ppermute(edge, ('cols', 'chan'), to_side)  9.05 us
    ppermute x1, waiting for transfers between devices, shards(): ours = lax.ppermute(edge, ('cols', 'chan'), to_side)  6.54 us
    pallas_call x1, Pallas kernels, shards(): pl.pallas_call(home_kernel, out_shape=tile, in_specs=specs(SMEM, SMEM, pl...  5.28 us
    all_to_all x1, starting transfers between devices, shards(): lax.all_to_all(gram, 'chan', split_axis=0, concat_axis=0, tiled=True)  4.91 us
    pallas_call x1, Pallas kernels, shards(): pl.pallas_call(lambda *refs: gram_kernel(tile_cols, *refs), out_shape=(ja...  4.7 us
    pallas_call x1, Pallas kernels, shards(): pl.pallas_call(radiance_kernel, out_shape=jax.ShapeDtypeStruct((members,...  4.03 us
    ppermute x1, starting transfers between devices, shards(): theirs = lax.ppermute(ours, 'chan', [(j, j ^ 1) for j in range(chans)])  3.12 us
  transfers between devices with their start and end apart: 4, of which 2 were waited for; matrix products, arithmetic and copies ran while one was open for 1% of the time, Pallas kernels for 22%

profile of v4, /device:TPU:1, one launch (start us, length us, event | category | flops | bytes accessed | tf_op | source)
XLA Modules:
  0.0 63.8 jit_solution(1014180049374361593)
XLA Ops:
  0.6 0.0 copy-start.3
  0.6 0.0 copy-start.4
  0.6 2.8 %prepare.1 = (bf16[32,80,128]{2,1,0:T(8,128)(2,1)}, bf16[8,16,32,128]{3,2,1,0:T(8,128)(2,1)}) custom-call(bf16[256,80,128]{2,1,0:T(8,128)(2,1)} %anomaly.3, bf16[16,256,128]{2,1,0:T(8,128)(2,1)} %refs_6_.1), custom_call_target="tpu_custom_call" | custom-call | flops 1000000 | bytes 3000000 | tf_op jit(solution)/shard_map/prepare/pallas_call | solution.py:244
  3.5 17.6 %all-to-all-start = ((bf16[8,16,32,128]{3,2,1,0:T(8,128)(2,1)}), bf16[8,16,32,128]{3,2,1,0:T(8,128)(2,1)S(1)}, u32[]{:S(2)}, u32[]{:S(2)}) async-start(bf16[8,16,32,128]{3,2,1,0:T(8,128)(2,1)} %get-tuple-element.6), calls=%async_computation | async-start | bytes 2097152 | tf_op jit(solution)/shard_map/all_to_all | solution.py:271
  21.1 9.1 %collective-permute-start = (bf16[32,80,128]{2,1,0:T(8,128)(2,1)}, bf16[32,80,128]{2,1,0:T(8,128)(2,1)S(1)}, u32[]{:S(2)}, u32[]{:S(2)}) collective-permute-start(bf16[32,80,128]{2,1,0:T(8,128)(2,1)} %get-tuple-element.7), channel_id=1, source_target_pairs={{0,8},{1,1017},{2,10},{3,1019},{4,12},{5,1021},{6,14},{7,1023},{8,... | collective-permute-start | bytes 1966088 | tf_op jit(solution)/shard_map/ppermute | solution.py:268
  30.2 0.0 copy-done.3
  30.2 0.0 copy-done.4
  30.2 0.1 dynamic_slice.3
  30.3 0.1 multiply_add_fusion.1
  31.1 0.1 add.70
  31.1 0.1 sub.50
  31.2 0.1 div.30
  31.3 0.1 concatenate.6.ints.refs_1_
  31.4 6.5 %collective-permute-done.refs_3_ = bf16[32,80,128]{2,1,0:T(8,128)(2,1)S(1)} collective-permute-done((bf16[32,80,128]{2,1,0:T(8,128)(2,1)}, bf16[32,80,128]{2,1,0:T(8,128)(2,1)S(1)}, u32[]{:S(2)}, u32[]{:S(2)}) %collective-permute-start) | collective-permute-done | bytes 655392 | tf_op jit(solution)/shard_map/ppermute | solution.py:268
  38.0 3.1 %collective-permute-start.1 = (bf16[32,80,128]{2,1,0:T(8,128)(2,1)S(1)}, bf16[32,80,128]{2,1,0:T(8,128)(2,1)S(1)}, u32[]{:S(2)}, u32[]{:S(2)}) collective-permute-start(bf16[32,80,128]{2,1,0:T(8,128)(2,1)S(1)} %collective-permute-done.refs_3_), channel_id=1, source_target_pairs={{0,1},{1,0},{2,3},{3,2},{4,5},{5,4},{6,7},{7,6},{8,9},{9,8},{10,11... | collective-permute-start | bytes 1966088 | tf_op jit(solution)/shard_map/ppermute | solution.py:269
  41.1 0.0 copy-start
  41.1 0.0 copy-start.1
  41.2 5.3 %home_mix.1.refs_5_ = bf16[128,80,128]{2,1,0:T(8,128)(2,1)S(1)} custom-call(s32[1154]{0:T(1024)S(1)} %concatenate.6.ints.refs_1_, f32[1152]{0:T(1024)S(1)} %pad_maximum_fusion.gains.refs_2_, bf16[256,80,128]{2,1,0:T(8,128)(2,1)} %anomaly.3), custom_call_target="tpu_custom_call" | custom-call | flops 4000000000 | bytes 8000000 | tf_op jit(solution)/shard_map/home_mix/pallas_call | solution.py:301
  46.4 0.0 collective-permute-done.1.refs_4_
  46.5 0.0 copy-done
  46.5 0.0 copy-done.1
  46.5 4.7 %gram.1 = (bf16[80,8,80]{2,1,0:T(8,128)(2,1)}, bf16[128,80,128]{2,1,0:T(8,128)(2,1)S(1)}) custom-call(s32[1]{0:T(128)S(6)} %copy.8.refs_0_.count, s32[1154]{0:T(1024)S(1)} %concatenate.6.ints.refs_1_, f32[1152]{0:T(1024)S(1)} %pad_maximum_fusion.gains.refs_2_, bf16[32,80,128]{2,1,0:T(8,128)(2,1)S(1)} %collective-permute-done.refs_3_, ...), custom_call_target="tpu_custom_call" | custom-call | flops 6000000000 | bytes 3000000 | tf_op jit(solution)/shard_map/gram/pallas_call | solution.py:312
  51.2 0.0 copy-start.2
  51.2 1.5 %copy-done.2 = bf16[128,80,128]{2,1,0:T(8,128)(2,1)} copy-done((bf16[128,80,128]{2,1,0:T(8,128)(2,1)}, bf16[128,80,128]{2,1,0:T(8,128)(2,1)S(1)}, u32[]{:S(2)}) %copy-start.2) | copy-done | bytes 2621464
  52.7 0.0 all-to-all-done
  52.7 4.9 %all-to-all-start.1 = ((bf16[80,8,80]{2,1,0:T(8,128)(2,1)}), bf16[80,8,80]{2,1,0:T(8,128)(2,1)S(1)}, u32[]{:S(2)}, u32[]{:S(2)}) async-start(bf16[80,8,80]{2,1,0:T(8,128)(2,1)} %get-tuple-element.9), calls=%async_computation.1 | async-start | bytes 327680 | tf_op jit(solution)/shard_map/all_to_all | solution.py:328
  57.6 4.0 %radiance.1 = bf16[80,32,128]{2,1,0:T(8,128)(2,1)} custom-call(s32[1]{0:T(128)S(6)} %copy.8.refs_0_.count, bf16[128,32,128]{2,1,0:T(8,128)(2,1)S(1)} %bitcast.26, bf16[128,80,128]{2,1,0:T(8,128)(2,1)} %copy-done.2), custom_call_target="tpu_custom_call" | custom-call | flops 4000000000 | bytes 5000000 | tf_op jit(solution)/shard_map/radiance/pallas_call | solution.py:329
  61.6 1.5 %all-to-all-done.1 = bf16[80,8,80]{2,1,0:T(8,128)(2,1)S(1)} async-done(((bf16[80,8,80]{2,1,0:T(8,128)(2,1)}), bf16[80,8,80]{2,1,0:T(8,128)(2,1)S(1)}, u32[]{:S(2)}, u32[]{:S(2)}) %all-to-all-start.1) | async-done | bytes 102432 | tf_op jit(solution)/shard_map/all_to_all | solution.py:328
  63.2 0.7 %convert_reduce_fusion = f32[10,8,80]{2,1,0:T(8,128)} fusion(bf16[8,10,8,80]{3,2,1,0:T(8,128)(2,1)S(1)} %bitcast.28), kind=kLoop, calls=%fused_computation | loop fusion | flops 96000 | bytes 128000 | tf_op jit(solution)/shard_map/reduce_sum | solution.py:344
  (9 shorter events, 0.1 us)
Async XLA Ops:
  0.6 29.5 %copy-start.3 = (f32[128,4]{0,1:T(4,128)S(1)}, f32[128,4]{0,1:T(4,128)}, u32[]{:S(2)}) copy-start(f32[128,4]{0,1:T(4,128)} %param.9) | copy-start | bytes 6148
  0.6 29.6 %copy-start.4 = (s32[128,4]{0,1:T(4,128)S(1)}, s32[128,4]{0,1:T(4,128)}, u32[]{:S(2)}) copy-start(s32[128,4]{0,1:T(4,128)} %param.8) | copy-start | bytes 6148
  3.5 49.2 %all-to-all-start = ((bf16[8,16,32,128]{3,2,1,0:T(8,128)(2,1)}), bf16[8,16,32,128]{3,2,1,0:T(8,128)(2,1)S(1)}, u32[]{:S(2)}, u32[]{:S(2)}) async-start(bf16[8,16,32,128]{3,2,1,0:T(8,128)(2,1)} %get-tuple-element.6), calls=%async_computation | async-start | bytes 2097152 | tf_op jit(solution)/shard_map/all_to_all | solution.py:271
  21.1 16.9 %collective-permute-start = (bf16[32,80,128]{2,1,0:T(8,128)(2,1)}, bf16[32,80,128]{2,1,0:T(8,128)(2,1)S(1)}, u32[]{:S(2)}, u32[]{:S(2)}) collective-permute-start(bf16[32,80,128]{2,1,0:T(8,128)(2,1)} %get-tuple-element.7), channel_id=1, source_target_pairs={{0,8},{1,1017},{2,10},{3,1019},{4,12},{5,1021},{6,14},{7,1023},{8,... | collective-permute-start | bytes 1966088 | tf_op jit(solution)/shard_map/ppermute | solution.py:268
  38.0 8.5 %collective-permute-start.1 = (bf16[32,80,128]{2,1,0:T(8,128)(2,1)S(1)}, bf16[32,80,128]{2,1,0:T(8,128)(2,1)S(1)}, u32[]{:S(2)}, u32[]{:S(2)}) collective-permute-start(bf16[32,80,128]{2,1,0:T(8,128)(2,1)S(1)} %collective-permute-done.refs_3_), channel_id=1, source_target_pairs={{0,1},{1,0},{2,3},{3,2},{4,5},{5,4},{6,7},{7,6},{8,9},{9,8},{10,11... | collective-permute-start | bytes 1966088 | tf_op jit(solution)/shard_map/ppermute | solution.py:269
  41.1 5.3 %copy-start = (bf16[16,256,128]{2,1,0:T(8,128)(2,1)S(1)}, bf16[16,256,128]{2,1,0:T(8,128)(2,1)}, u32[]{:S(2)}) copy-start(bf16[16,256,128]{2,1,0:T(8,128)(2,1)} %refs_6_.1) | copy-start | bytes 3145732
  41.1 5.3 %copy-start.1 = (bf16[256,16]{0,1:T(8,128)(2,1)S(1)}, bf16[256,16]{0,1:T(8,128)(2,1)}, u32[]{:S(2)}) copy-start(bf16[256,16]{0,1:T(8,128)(2,1)} %param.11) | copy-start | bytes 24580
  51.2 1.5 %copy-start.2 = (bf16[128,80,128]{2,1,0:T(8,128)(2,1)}, bf16[128,80,128]{2,1,0:T(8,128)(2,1)S(1)}, u32[]{:S(2)}) copy-start(bf16[128,80,128]{2,1,0:T(8,128)(2,1)S(1)} %get-tuple-element.8.mixed_ref) | copy-start | bytes 7864324
  52.7 10.5 %all-to-all-start.1 = ((bf16[80,8,80]{2,1,0:T(8,128)(2,1)}), bf16[80,8,80]{2,1,0:T(8,128)(2,1)S(1)}, u32[]{:S(2)}, u32[]{:S(2)}) async-start(bf16[80,8,80]{2,1,0:T(8,128)(2,1)} %get-tuple-element.9), calls=%async_computation.1 | async-start | bytes 327680 | tf_op jit(solution)/shard_map/all_to_all | solution.py:328

commit v5 on v4

--- a/solution.py
+++ b/solution.py
@@ -17,6 +17,7 @@
 HOME_COLS = TAIL + 2
 LOCALITY = FP * OBS_DEV
 HOME_GAINS = LOCALITY + OBS_DEV
+LIVE = HOME_GAINS + FP * OBS_DEV
 
 VMEM = pltpu.MemorySpace.VMEM
 SMEM = pltpu.MemorySpace.SMEM
@@ -100,10 +101,9 @@
         lax.fori_loop(0, OBS_DEV, each, 0, unroll=4)
 
 
-def gram_kernel(tile_cols, count, ints, gains, ours, theirs, home, jac, weight, gram, mixed_out, mixed, perts, products, turned, sem):
+def gram_kernel(tile_cols, ints, gains, ours, theirs, home, jac, weight, gram, mixed_out, mixed, perts, products, turned, sem):
     share, members = perts.shape[:2]
     first_obs = ints[TAIL]
-    live_count = count[0]
     first_ours = ints[TAIL + 1]
     first_theirs = HALO + tile_cols - first_ours
 
@@ -136,7 +136,7 @@
     leave = pltpu.make_async_copy(mixed, mixed_out, sem)
     leave.start()
     for i in range(share):
-        live = jnp.where(first_obs + i < live_count, 1.0, 0.0)
+        live = gains[LIVE + first_obs + i]
         radiance = lax.dot_general(
             mixed[first_obs + i], jac[i], NT, preferred_element_type=jnp.float32
         )
@@ -157,7 +157,7 @@
     leave.wait()
 
 
-def radiance_kernel(count, jac, mixed_ref, out, mixed, turned, sems):
+def radiance_kernel(alive, jac, mixed_ref, out, mixed, turned, sems):
     members, block, levels = mixed.shape[1], jac.shape[1], jac.shape[2]
     steps = sems.shape[0]
     packs = levels // block
@@ -198,7 +198,7 @@
         lax.fori_loop(step * batch, (step + 1) * batch, group, 0, unroll=batch)
     slot = lax.broadcasted_iota(jnp.int32, (block, OBS_DEV), 1)
     spot = slot // groups
-    live = slot < count[0]
+    live = jnp.broadcast_to(alive[...], slot.shape) > 0.0
 
     def members_of(q, carry):
         rows = [
@@ -293,8 +293,9 @@
     home_cols = jnp.clip(offsets - HALO, 0, tile_cols - 1)
     home_gains = jnp.where(inside, column_gains, 0.0)
     ints = jnp.concatenate([offsets.reshape(-1), reach, tail, home_cols.reshape(-1)])
+    alive = (jnp.arange(OBS_DEV, dtype=jnp.int32) < obs_count[0]).astype(jnp.float32)
     gains = jnp.concatenate(
-        [column_gains.reshape(-1), locality.reshape(-1), home_gains.reshape(-1)]
+        [column_gains.reshape(-1), locality.reshape(-1), home_gains.reshape(-1), alive]
     )
 
     tile = jax.ShapeDtypeStruct((OBS_DEV, members, levels), jnp.bfloat16)
@@ -312,7 +313,7 @@
     gram, mixed = pl.pallas_call(
         lambda *refs: gram_kernel(tile_cols, *refs),
         out_shape=(jax.ShapeDtypeStruct((members, PTS, members), jnp.bfloat16), tile),
-        in_specs=specs(SMEM, SMEM, SMEM, VMEM, VMEM, VMEM, VMEM, VMEM),
+        in_specs=specs(SMEM, SMEM, VMEM, VMEM, VMEM, VMEM, VMEM),
         out_specs=tuple(specs(VMEM, pl.ANY)),
         scratch_shapes=[
             pltpu.VMEM(tile.shape, tile.dtype),
@@ -324,12 +325,12 @@
         compiler_params=params(46),
         cost_estimate=cost(6_000_000_000, 3_000_000),
         name="gram",
-    )(obs_count, ints, gains, ours, theirs, home, jacobian, obs_weight.T)
+    )(ints, gains, ours, theirs, home, jacobian, obs_weight.T)
     arrived = lax.all_to_all(gram, "chan", split_axis=0, concat_axis=0, tiled=True)
     perturbed = pl.pallas_call(
         radiance_kernel,
         out_shape=jax.ShapeDtypeStruct((members, block, OBS_DEV), jnp.bfloat16),
-        in_specs=specs(SMEM, VMEM, pl.ANY),
+        in_specs=specs(VMEM, VMEM, pl.ANY),
         out_specs=pl.BlockSpec(memory_space=VMEM),
         scratch_shapes=[
             pltpu.VMEM(tile.shape, tile.dtype),
@@ -339,7 +340,7 @@
         compiler_params=params(52),
         cost_estimate=cost(4_000_000_000, 5_000_000),
         name="radiance",
-    )(obs_count, jac_block, mixed)
+    )(alive[None], jac_block, mixed)
 
     gram_rows = arrived.reshape(chans, members // chans, PTS, members).astype(jnp.float32).sum(0)
     return perturbed, gram_rows.transpose(1, 0, 2)

time: 64.2 us -> 64.2 us (level)
  no operation moved by 1% of the time
where the time goes in v5:
time: 64.2 us; the launch traced here: 63.8 us
  starting transfers between devices  34.7 us (54%)
  Pallas kernels  16.9 us (26%)
  waiting for transfers between devices  8.05 us (13%)
  local copies, waits for them, and re-layouts  1.93 us (3%)
  between operations  1.46 us (2%)
  other arithmetic  0.86 us (1%)
    all_to_all x1, starting transfers between devices, shards(): lax.all_to_all(pieces, 'chan', split_axis=0, concat_axis=0, tiled=True)  17.6 us
    ppermute x1, starting transfers between devices, shards(): ours = lax.ppermute(edge, ('cols', 'chan'), to_side)  9.05 us
    ppermute x1, waiting for transfers between devices, shards(): ours = lax.ppermute(edge, ('cols', 'chan'), to_side)  6.53 us
    pallas_call x1, Pallas kernels, shards(): pl.pallas_call(home_kernel, out_shape=tile, in_specs=specs(SMEM, SMEM, pl...  5.29 us
    all_to_all x1, starting transfers between devices, shards(): lax.all_to_all(gram, 'chan', split_axis=0, concat_axis=0, tiled=True)  4.92 us
    pallas_call x1, Pallas kernels, shards(): pl.pallas_call(lambda *refs: gram_kernel(tile_cols, *refs), out_shape=(ja...  4.7 us
    pallas_call x1, Pallas kernels, shards(): pl.pallas_call(radiance_kernel, out_shape=jax.ShapeDtypeStruct((members,...  4.03 us
    ppermute x1, starting transfers between devices, shards(): theirs = lax.ppermute(ours, 'chan', [(j, j ^ 1) for j in range(chans)])  3.12 us
  transfers between devices with their start and end apart: 4, of which 2 were waited for; matrix products, arithmetic and copies ran while one was open for 1% of the time, Pallas kernels for 22%

profile of v5, /device:TPU:1, one launch (start us, length us, event | category | flops | bytes accessed | tf_op | source)
XLA Modules:
  0.0 63.8 jit_solution(201532067277950530)
XLA Ops:
  0.6 0.0 copy-start.3
  0.6 0.0 copy-start.4
  0.6 2.8 %prepare.1 = (bf16[32,80,128]{2,1,0:T(8,128)(2,1)}, bf16[8,16,32,128]{3,2,1,0:T(8,128)(2,1)}) custom-call(bf16[256,80,128]{2,1,0:T(8,128)(2,1)} %anomaly.3, bf16[16,256,128]{2,1,0:T(8,128)(2,1)} %refs_5_.1), custom_call_target="tpu_custom_call" | custom-call | flops 1000000 | bytes 3000000 | tf_op jit(solution)/shard_map/prepare/pallas_call | solution.py:244
  3.5 17.6 %all-to-all-start = ((bf16[8,16,32,128]{3,2,1,0:T(8,128)(2,1)}), bf16[8,16,32,128]{3,2,1,0:T(8,128)(2,1)S(1)}, u32[]{:S(2)}, u32[]{:S(2)}) async-start(bf16[8,16,32,128]{3,2,1,0:T(8,128)(2,1)} %get-tuple-element.6), calls=%async_computation | async-start | bytes 2097152 | tf_op jit(solution)/shard_map/all_to_all | solution.py:271
  21.1 9.1 %collective-permute-start = (bf16[32,80,128]{2,1,0:T(8,128)(2,1)}, bf16[32,80,128]{2,1,0:T(8,128)(2,1)S(1)}, u32[]{:S(2)}, u32[]{:S(2)}) collective-permute-start(bf16[32,80,128]{2,1,0:T(8,128)(2,1)} %get-tuple-element.7), channel_id=1, source_target_pairs={{0,8},{1,1017},{2,10},{3,1019},{4,12},{5,1021},{6,14},{7,1023},{8,... | collective-permute-start | bytes 1966088 | tf_op jit(solution)/shard_map/ppermute | solution.py:268
  30.8 0.0 copy-done.3
  30.8 0.0 copy-done.4
  30.9 0.1 dynamic_slice.3
  31.0 0.1 multiply_add_fusion.1
  31.1 0.1 add.70
  31.2 0.1 sub.50
  31.2 0.1 div.30
  31.3 0.1 concatenate.6.ints.refs_0_
  31.4 6.5 %collective-permute-done.refs_2_ = bf16[32,80,128]{2,1,0:T(8,128)(2,1)S(1)} collective-permute-done((bf16[32,80,128]{2,1,0:T(8,128)(2,1)}, bf16[32,80,128]{2,1,0:T(8,128)(2,1)S(1)}, u32[]{:S(2)}, u32[]{:S(2)}) %collective-permute-start) | collective-permute-done | bytes 655392 | tf_op jit(solution)/shard_map/ppermute | solution.py:268
  38.0 3.1 %collective-permute-start.1 = (bf16[32,80,128]{2,1,0:T(8,128)(2,1)S(1)}, bf16[32,80,128]{2,1,0:T(8,128)(2,1)S(1)}, u32[]{:S(2)}, u32[]{:S(2)}) collective-permute-start(bf16[32,80,128]{2,1,0:T(8,128)(2,1)S(1)} %collective-permute-done.refs_2_), channel_id=1, source_target_pairs={{0,1},{1,0},{2,3},{3,2},{4,5},{5,4},{6,7},{7,6},{8,9},{9,8},{10,11... | collective-permute-start | bytes 1966088 | tf_op jit(solution)/shard_map/ppermute | solution.py:269
  41.1 0.0 copy-start
  41.1 0.0 copy-start.1
  41.2 5.3 %home_mix.1.refs_4_ = bf16[128,80,128]{2,1,0:T(8,128)(2,1)S(1)} custom-call(s32[1154]{0:T(1024)S(1)} %concatenate.6.ints.refs_0_, f32[1280]{0:T(1024)S(1)} %pad_maximum_fusion.gains.refs_1_, bf16[256,80,128]{2,1,0:T(8,128)(2,1)} %anomaly.3), custom_call_target="tpu_custom_call" | custom-call | flops 4000000000 | bytes 8000000 | tf_op jit(solution)/shard_map/home_mix/pallas_call | solution.py:302
  46.5 0.0 collective-permute-done.1.refs_3_
  46.5 0.0 copy-done
  46.5 0.0 copy-done.1
  46.5 4.7 %gram.1 = (bf16[80,8,80]{2,1,0:T(8,128)(2,1)}, bf16[128,80,128]{2,1,0:T(8,128)(2,1)S(1)}) custom-call(s32[1154]{0:T(1024)S(1)} %concatenate.6.ints.refs_0_, f32[1280]{0:T(1024)S(1)} %pad_maximum_fusion.gains.refs_1_, bf16[32,80,128]{2,1,0:T(8,128)(2,1)S(1)} %collective-permute-done.refs_2_, bf16[32,80,128]{2,1,0:T(8,128)(2,1)S(1)} %collective-permute-done.1.refs_3_, ...), custom_call_target="tpu_custom_call" | custom-call | flops 6000000000 | bytes 3000000 | tf_op jit(solution)/shard_map/gram/pallas_call | solution.py:313
  51.2 0.0 copy-start.2
  51.2 1.5 %copy-done.2 = bf16[128,80,128]{2,1,0:T(8,128)(2,1)} copy-done((bf16[128,80,128]{2,1,0:T(8,128)(2,1)}, bf16[128,80,128]{2,1,0:T(8,128)(2,1)S(1)}, u32[]{:S(2)}) %copy-start.2) | copy-done | bytes 2621464
  52.7 0.0 all-to-all-done
  52.7 4.9 %all-to-all-start.1 = ((bf16[80,8,80]{2,1,0:T(8,128)(2,1)}), bf16[80,8,80]{2,1,0:T(8,128)(2,1)S(1)}, u32[]{:S(2)}, u32[]{:S(2)}) async-start(bf16[80,8,80]{2,1,0:T(8,128)(2,1)} %get-tuple-element.9), calls=%async_computation.1 | async-start | bytes 327680 | tf_op jit(solution)/shard_map/all_to_all | solution.py:329
  57.6 4.0 %radiance.1 = bf16[80,32,128]{2,1,0:T(8,128)(2,1)} custom-call(f32[1,128]{1,0:T(1,128)S(1)} %compare_convert_fusion.1.alive, bf16[128,32,128]{2,1,0:T(8,128)(2,1)S(1)} %bitcast.29, bf16[128,80,128]{2,1,0:T(8,128)(2,1)} %copy-done.2), custom_call_target="tpu_custom_call" | custom-call | flops 4000000000 | bytes 5000000 | tf_op jit(solution)/shard_map/radiance/pallas_call | solution.py:330
  61.7 1.5 %all-to-all-done.1 = bf16[80,8,80]{2,1,0:T(8,128)(2,1)S(1)} async-done(((bf16[80,8,80]{2,1,0:T(8,128)(2,1)}), bf16[80,8,80]{2,1,0:T(8,128)(2,1)S(1)}, u32[]{:S(2)}, u32[]{:S(2)}) %all-to-all-start.1) | async-done | bytes 102432 | tf_op jit(solution)/shard_map/all_to_all | solution.py:329
  63.2 0.7 %convert_reduce_fusion = f32[10,8,80]{2,1,0:T(8,128)} fusion(bf16[8,10,8,80]{3,2,1,0:T(8,128)(2,1)S(1)} %bitcast.31), kind=kLoop, calls=%fused_computation | loop fusion | flops 96000 | bytes 128000 | tf_op jit(solution)/shard_map/reduce_sum | solution.py:345
  (11 shorter events, 0.1 us)
Async XLA Ops:
  0.6 30.2 %copy-start.3 = (f32[128,4]{0,1:T(4,128)S(1)}, f32[128,4]{0,1:T(4,128)}, u32[]{:S(2)}) copy-start(f32[128,4]{0,1:T(4,128)} %param.9) | copy-start | bytes 6148
  0.6 30.2 %copy-start.4 = (s32[128,4]{0,1:T(4,128)S(1)}, s32[128,4]{0,1:T(4,128)}, u32[]{:S(2)}) copy-start(s32[128,4]{0,1:T(4,128)} %param.8) | copy-start | bytes 6148
  3.5 49.2 %all-to-all-start = ((bf16[8,16,32,128]{3,2,1,0:T(8,128)(2,1)}), bf16[8,16,32,128]{3,2,1,0:T(8,128)(2,1)S(1)}, u32[]{:S(2)}, u32[]{:S(2)}) async-start(bf16[8,16,32,128]{3,2,1,0:T(8,128)(2,1)} %get-tuple-element.6), calls=%async_computation | async-start | bytes 2097152 | tf_op jit(solution)/shard_map/all_to_all | solution.py:271
  21.1 16.9 %collective-permute-start = (bf16[32,80,128]{2,1,0:T(8,128)(2,1)}, bf16[32,80,128]{2,1,0:T(8,128)(2,1)S(1)}, u32[]{:S(2)}, u32[]{:S(2)}) collective-permute-start(bf16[32,80,128]{2,1,0:T(8,128)(2,1)} %get-tuple-element.7), channel_id=1, source_target_pairs={{0,8},{1,1017},{2,10},{3,1019},{4,12},{5,1021},{6,14},{7,1023},{8,... | collective-permute-start | bytes 1966088 | tf_op jit(solution)/shard_map/ppermute | solution.py:268
  38.0 8.5 %collective-permute-start.1 = (bf16[32,80,128]{2,1,0:T(8,128)(2,1)S(1)}, bf16[32,80,128]{2,1,0:T(8,128)(2,1)S(1)}, u32[]{:S(2)}, u32[]{:S(2)}) collective-permute-start(bf16[32,80,128]{2,1,0:T(8,128)(2,1)S(1)} %collective-permute-done.refs_2_), channel_id=1, source_target_pairs={{0,1},{1,0},{2,3},{3,2},{4,5},{5,4},{6,7},{7,6},{8,9},{9,8},{10,11... | collective-permute-start | bytes 1966088 | tf_op jit(solution)/shard_map/ppermute | solution.py:269
  41.1 5.3 %copy-start = (bf16[16,256,128]{2,1,0:T(8,128)(2,1)S(1)}, bf16[16,256,128]{2,1,0:T(8,128)(2,1)}, u32[]{:S(2)}) copy-start(bf16[16,256,128]{2,1,0:T(8,128)(2,1)} %refs_5_.1) | copy-start | bytes 3145732
  41.1 5.3 %copy-start.1 = (bf16[256,16]{0,1:T(8,128)(2,1)S(1)}, bf16[256,16]{0,1:T(8,128)(2,1)}, u32[]{:S(2)}) copy-start(bf16[256,16]{0,1:T(8,128)(2,1)} %param.11) | copy-start | bytes 24580
  51.2 1.5 %copy-start.2 = (bf16[128,80,128]{2,1,0:T(8,128)(2,1)}, bf16[128,80,128]{2,1,0:T(8,128)(2,1)S(1)}, u32[]{:S(2)}) copy-start(bf16[128,80,128]{2,1,0:T(8,128)(2,1)S(1)} %get-tuple-element.8.mixed_ref) | copy-start | bytes 7864324
  52.7 10.5 %all-to-all-start.1 = ((bf16[80,8,80]{2,1,0:T(8,128)(2,1)}), bf16[80,8,80]{2,1,0:T(8,128)(2,1)S(1)}, u32[]{:S(2)}, u32[]{:S(2)}) async-start(bf16[80,8,80]{2,1,0:T(8,128)(2,1)} %get-tuple-element.9), calls=%async_computation.1 | async-start | bytes 327680 | tf_op jit(solution)/shard_map/all_to_all | solution.py:329
